TPU v7x, 512 devices: a 4x2x32 block of a 4x8x32 slice. The times are simulated.
512 devices in a mesh: groups: 2 (over y), rows: 64 (over z, core), cols: 4 (over x).
Axes of the slice: x: 4, y: 2, z: 32, core: 2. Of those that a mesh axis runs over, the one named last changes fastest.
The devices are a block of a 4x8x32 slice.
Arguments:
- alignment_features: float32 [2048, 32, 64], P(('groups', 'rows'), 'cols'), parts along dimension 0, may hold values from -6 to 6
- affine_factor: float32 [64], replicated, may hold values from 0.25 to 1.75
- affine_offset: float32 [64], replicated, may hold values from -3 to 3
- first_projector: bfloat16 [64, 32], replicated, may hold values from -0.75 to 0.75
- second_projector: bfloat16 [64, 32], replicated, may hold values from -0.75 to 0.75
- final_projector: bfloat16 [1024, 128], replicated, may hold values from -0.75 to 0.75
- additive_term: float32 [128], replicated, may hold values from -3 to 3
- adjoint_update: bfloat16 [2048, 1024, 128], P(('groups', 'rows'), 'cols'), parts along dimension 0, may hold values from -6 to 6
Outputs:
- residue_update: bfloat16 [2048, 1024, 128], P(('groups', 'rows'), 'cols'), parts along dimension 0
- alignment_slope: float32 [2048, 32, 64], P(('groups', 'rows'), 'cols'), parts along dimension 0
- final_projector_slope: float32 [2048, 128], P(('groups', 'rows', 'cols')), parts along dimension 0
- first_projector_slope: float32 [128, 32], P('groups'), parts along dimension 0
- second_projector_slope: float32 [128, 32], P('groups'), parts along dimension 0
There are 2 independent parts, one for each index of `groups`. A program takes and returns all parts, laid end to end along the dimension named above; an argument that names none is the same for every part. Nothing has to cross between parts.
All inputs are finite; a program needn't handle non-finite values.
Results may differ from a plain program's by a relative error of at most 0.0061.
Values may be sent and summed in bfloat16 or wider, within the bound.
A program may use at most 64 MiB of HBM per device.

v0:
```python
import jax
import jax.numpy as jnp
from jax import lax
from jax.sharding import Mesh
from jax.sharding import PartitionSpec as P

ROWS = ("rows_0", "rows_1")
ROWS_COLS = ("rows_0", "rows_1", "cols")
GROUPS_ROWS = ("groups", "rows_0", "rows_1")
GROUPS_ROWS_COLS = ("groups", "rows_0", "rows_1", "cols")


def joined_along(pieces, dim):
    dims = list(pieces.shape[1:])
    dims[dim] *= pieces.shape[0]
    return jnp.moveaxis(pieces, 0, dim).reshape(dims)


def sent_to_all(array, axis):
    copies = jnp.broadcast_to(array, (lax.axis_size(axis), *array.shape))
    return lax.all_to_all(copies, axis, split_axis=0, concat_axis=0, tiled=True)


def gathered_copies(array, axis, dim):
    return joined_along(sent_to_all(array, axis), dim)


def gather_in_order(array, axes, turns):
    pieces = array[None]
    for k in turns:
        pieces = lax.all_gather(pieces, axes[k], axis=0, tiled=True)
    current = [lax.axis_size(axes[k]) for k in reversed(turns)]
    pieces = pieces.reshape(*current, *array.shape)
    turned = sorted(range(len(turns)), key=lambda place: turns[len(turns) - 1 - place])
    return pieces.transpose(*turned, *range(len(turns), pieces.ndim)).reshape(-1, *array.shape)


def gather_axes(array, axes, turns, dim):
    return joined_along(gather_in_order(array, axes, turns), dim)


def cut_along(array, dim, peers):
    dims = array.shape
    pieces = array.reshape(*dims[:dim], peers, dims[dim] // peers, *dims[dim + 1 :])
    return jnp.moveaxis(pieces, dim, 0)


def sent_and_summed(array, axis, dim):
    peers = lax.axis_size(axis)
    pieces = lax.all_to_all(cut_along(array, dim, peers), axis, 0, 0, tiled=True)
    return jnp.sum(pieces, axis=0)


def sum_at_owner(array, axis, dim):
    pieces = cut_along(array, dim, lax.axis_size(axis))
    arrived = lax.all_to_all(pieces, axis, split_axis=0, concat_axis=0, tiled=True)
    return arrived.astype(jnp.float32).sum(axis=0)


def one_axis_at_a_time(array, axes):
    for axis in axes:
        array = lax.psum(array, axis)
    return array


def layernorm_parts(alignment_features, affine_factor, affine_offset):
    centered_alignment = alignment_features - jnp.mean(alignment_features, axis=-1, keepdims=True)
    reciprocal_spread = lax.rsqrt(
        jnp.mean(centered_alignment * centered_alignment, axis=-1, keepdims=True) + 1e-05
    )
    zscored_alignment = centered_alignment * reciprocal_spread
    return (
        zscored_alignment,
        reciprocal_spread,
        (zscored_alignment * affine_factor + affine_offset).astype(jnp.bfloat16),
    )


def local(
    alignment_features,
    affine_factor,
    affine_offset,
    first_projector,
    second_projector,
    final_projector,
    additive_term,
    adjoint_update,
):
    zscored_alignment, reciprocal_spread, unit_alignment = layernorm_parts(
        alignment_features, affine_factor, affine_offset
    )
    first_factor_here = jnp.dot(
        unit_alignment, first_projector, preferred_element_type=jnp.float32
    ).astype(jnp.bfloat16)
    second_factor_here = jnp.dot(
        unit_alignment, second_projector, preferred_element_type=jnp.float32
    ).astype(jnp.bfloat16)
    tokens, quarter, chans = first_factor_here.shape
    left_flat = first_factor_here.reshape(tokens, quarter * chans)
    right_flat = second_factor_here.reshape(tokens, quarter * chans)
    left_rows = gathered_copies(left_flat, "cols", 1).reshape(tokens, -1, chans)
    right_all = gather_axes(right_flat, ROWS, (0, 1), 0)
    block = right_all.shape[0] // lax.axis_size("cols")
    right_cols = lax.all_to_all(right_all, "cols", split_axis=0, concat_axis=1, tiled=True).reshape(
        block, -1, chans
    )
    seqs = left_rows.shape[1]
    multiplier = 1.0 / seqs
    pair_ch = adjoint_update.shape[2]
    step_rows = 4
    rounds = tokens // step_rows
    first_tile_list = left_rows.reshape(rounds, step_rows, seqs, chans)
    cot_blocks = adjoint_update.reshape(rounds, step_rows, block, pair_ch)

    def advance(carry, inputs):
        right_acc, out_acc = carry
        left_slab, cot_slab = inputs
        outer = (
            jnp.einsum("isc,jsd->ijcd", left_slab, right_cols, preferred_element_type=jnp.float32)
            * multiplier
        ).astype(jnp.bfloat16)
        flat = outer.reshape(step_rows * block, chans * chans)
        cot_flat = cot_slab.reshape(step_rows * block, pair_ch)
        update = (
            jnp.dot(flat, final_projector, preferred_element_type=jnp.float32) + additive_term
        ).astype(jnp.bfloat16)
        outer_grad = jnp.dot(
            cot_flat, final_projector.T, preferred_element_type=jnp.float32
        ).astype(jnp.bfloat16)
        outer_grad = outer_grad.reshape(step_rows, block, chans, chans)
        left_piece = (
            jnp.einsum("ijcd,jsd->isc", outer_grad, right_cols, preferred_element_type=jnp.float32)
            * multiplier
        )
        right_acc = (
            right_acc
            + jnp.einsum("ijcd,isc->jsd", outer_grad, left_slab, preferred_element_type=jnp.float32)
            * multiplier
        )
        out_acc = out_acc + jnp.einsum(
            "fk,fe->ke", flat, cot_flat, preferred_element_type=jnp.float32
        )
        return ((right_acc, out_acc), (update.reshape(step_rows, block, pair_ch), left_piece))

    beginning_position = (
        jnp.zeros((block, seqs, chans), jnp.float32),
        jnp.zeros((chans * chans, pair_ch), jnp.float32),
    )
    (right_part, out_term), (updates, left_pieces) = lax.scan(
        advance, beginning_position, (first_tile_list, cot_blocks)
    )
    residue_update = updates.reshape(tokens, block, pair_ch)
    left_part = left_pieces.reshape(tokens, seqs * chans)
    first_adjoint = sent_and_summed(left_part, "cols", 1).reshape(tokens, quarter, chans)
    moved = lax.all_to_all(
        right_part.reshape(block, seqs * chans).astype(jnp.bfloat16),
        "cols",
        split_axis=1,
        concat_axis=0,
        tiled=True,
    )
    right_back = sum_at_owner(moved, ROWS, 0).reshape(tokens, quarter, chans)
    partial_sum = sum_at_owner(out_term.astype(jnp.bfloat16), ROWS, 0)
    final_projector_slope = sent_and_summed(partial_sum, "cols", 0)
    unit_broadcast = unit_alignment.astype(jnp.float32)
    high = lax.Precision.HIGHEST
    left_term = jnp.einsum("tsk,tsc->kc", unit_broadcast, first_adjoint, precision=high)
    right_term = jnp.einsum("tsk,tsc->kc", unit_broadcast, right_back, precision=high)
    first_projector_slope, second_projector_slope = (
        one_axis_at_a_time(left_term, ROWS_COLS),
        one_axis_at_a_time(right_term, ROWS_COLS),
    )
    unit_adjoint = jnp.einsum(
        "tsc,kc->tsk", first_adjoint, first_projector.astype(jnp.float32), precision=high
    )
    unit_adjoint = unit_adjoint + jnp.einsum(
        "tsc,kc->tsk", right_back, second_projector.astype(jnp.float32), precision=high
    )
    scaled_alignment = unit_adjoint * affine_factor
    alignment_slope = reciprocal_spread * (
        scaled_alignment
        - jnp.mean(scaled_alignment, axis=-1, keepdims=True)
        - zscored_alignment * jnp.mean(scaled_alignment * zscored_alignment, axis=-1, keepdims=True)
    )
    return (
        residue_update,
        alignment_slope,
        final_projector_slope,
        first_projector_slope,
        second_projector_slope,
    )


def solution(mesh):
    split = Mesh(
        mesh.devices.reshape(mesh.shape["groups"], 32, 2, mesh.shape["cols"]),
        ("groups", "rows_0", "rows_1", "cols"),
    )
    return jax.shard_map(
        local,
        mesh=split,
        in_specs=(
            P(GROUPS_ROWS, "cols", None),
            P(),
            P(),
            P(),
            P(),
            P(),
            P(),
            P(GROUPS_ROWS, "cols", None),
        ),
        out_specs=(
            P(GROUPS_ROWS, "cols", None),
            P(GROUPS_ROWS, "cols", None),
            P(GROUPS_ROWS_COLS, None),
            P("groups", None),
            P("groups", None),
        ),
        check_vma=False,
    )
```

profile of v0, /device:TPU:33, one launch (start us, length us, event | category | flops | bytes accessed | tf_op | source)
XLA Modules:
  0.0 482.3 jit_solution(18128070423771525346)
XLA Ops:
  5.2 5.1 %all-to-all-start = ((bf16[4,16,256]{2,1,0:T(8,128)(2,1)}), bf16[4,16,256]{2,1,0:T(8,128)(2,1)S(1)}, u32[]{:S(2)}, u32[]{:S(2)}) async-start(bf16[4,16,256]{2,1,0:T(8,128)(2,1)} %broadcast_in_dim.35), calls=%async_computation | async-start | bytes 65536 | tf_op jit(solution)/shard_map/all_to_all | solution.py:21
  10.6 82.1 %all_gather.6 = bf16[32,16,256]{2,1,0:T(8,128)(2,1)S(1)} all-gather(bf16[1,16,256]{2,1,0:T(8,128)(2,1)S(1)} %broadcast_in_dim_reshape.3), channel_id=1, replica_groups=mesh['groups'=2,'rows_0'=32,'rows_1'=2,'cols'=4] {'rows_0'}, dimensions={0}, use_global_device_ids=true | all-gather | bytes 270336 | tf_op jit(solution)/shard_map/all_gather | solution.py:31
  92.6 16.6 %all_gather.7 = bf16[64,16,256]{2,1,0:T(8,128)(2,1)S(1)} all-gather(bf16[32,16,256]{2,1,0:T(8,128)(2,1)S(1)} %all_gather.6), channel_id=1, replica_groups=mesh['groups'=2,'rows_0'=32,'rows_1'=2,'cols'=4] {'rows_1'}, dimensions={0}, use_global_device_ids=true | all-gather | bytes 786432 | tf_op jit(solution)/shard_map/all_gather | solution.py:31
  110.1 4.5 all-to-all-start.1
  115.4 8.1 %all-to-all-done.1 = bf16[4,256,256]{2,1,0:T(8,128)(2,1)S(1)} async-done(((bf16[4,256,256]{2,1,0:T(8,128)(2,1)}), bf16[4,256,256]{2,1,0:T(8,128)(2,1)S(1)}, u32[]{:S(2)}, u32[]{:S(2)}) %all-to-all-start.1) | async-done | bytes 524320 | tf_op jit(solution)/shard_map/all_to_all | solution.py:104
  124.8 83.5 %while.17 = (s32[]{:T(128)}, f32[256,32,32]{0,1,2:T(8,128)S(1)}, f32[1024,128]{1,0:T(8,128)}, bf16[4,4,256,128]{3,2,1,0:T(8,128)(2,1)}, f32[4,4,32,32]{3,2,1,0:T...) while((s32[]{:T(128)}, f32[256,32,32]{0,1,2:T(8,128)S(1)}, ...), condition=%wide.region_3.4_spmd.clone, body=%wide.region_2.3_spmd.clone.sunk | while | flops 1011093504 | bytes 36110996 | solution.py:149
  133.5 2.6 copy.230
  136.1 3.3 reshape.110
  139.4 2.5 fusion.88
  151.3 2.6 convolution_add_fusion.4
  154.6 2.6 copy.230
  157.2 3.3 reshape.110
  160.5 2.5 fusion.88
  172.5 2.6 convolution_add_fusion.4
  175.8 2.6 copy.230
  178.3 3.3 reshape.110
  193.6 2.6 convolution_add_fusion.4
  196.9 2.6 copy.230
  199.5 3.3 reshape.110
  210.1 3.4 all-to-all-start.2
  215.2 2.6 all-to-all-done.2
  217.8 8.2 %all-to-all-start.5 = ((bf16[64,16,128]{2,1,0:T(8,128)(2,1)}), bf16[64,16,128]{2,1,0:T(8,128)(2,1)S(1)}, u32[]{:S(2)}, u32[]{:S(2)}) async-start(bf16[64,16,128]{2,1,0:T(8,128)(2,1)} %bitcast.14), calls=%async_computation.5 | async-start | bytes 524288 | tf_op jit(solution)/shard_map/all_to_all | solution.py:56
  227.4 39.8 %all-to-all-done.5 = bf16[64,16,128]{2,1,0:T(8,128)(2,1)S(1)} async-done(((bf16[64,16,128]{2,1,0:T(8,128)(2,1)}), bf16[64,16,128]{2,1,0:T(8,128)(2,1)S(1)}, u32[]{:S(2)}, u32[]{:S(2)}) %all-to-all-start.5) | async-done | bytes 262176 | tf_op jit(solution)/shard_map/all_to_all | solution.py:56
  267.2 3.7 all-to-all-start.3
  271.6 6.6 %all-to-all-done.3 = bf16[256,4,256]{0,2,1:T(8,128)(2,1)S(1)} async-done(((bf16[256,4,256]{0,2,1:T(8,128)(2,1)}), bf16[256,4,256]{0,2,1:T(8,128)(2,1)S(1)}, u32[]{:S(2)}, u32[]{:S(2)}) %all-to-all-start.3) | async-done | bytes 524320 | tf_op jit(solution)/shard_map/all_to_all | solution.py:155
  278.2 3.3 all-to-all-start.6
  282.5 3.1 all-to-all-done.6
  285.6 9.1 %all-to-all-start.4 = ((bf16[64,16,256]{2,1,0:T(8,128)(2,1)}), bf16[64,16,256]{2,1,0:T(8,128)(2,1)S(1)}, u32[]{:S(2)}, u32[]{:S(2)}) async-start(bf16[64,16,256]{2,1,0:T(8,128)(2,1)} %bitcast.13), calls=%async_computation.4 | async-start | bytes 1048576 | tf_op jit(solution)/shard_map/all_to_all | solution.py:56
  295.8 61.8 %all-to-all-done.4 = bf16[64,16,256]{2,1,0:T(8,128)(2,1)S(1)} async-done(((bf16[64,16,256]{2,1,0:T(8,128)(2,1)}), bf16[64,16,256]{2,1,0:T(8,128)(2,1)S(1)}, u32[]{:S(2)}, u32[]{:S(2)}) %all-to-all-start.4) | async-done | bytes 524320 | tf_op jit(solution)/shard_map/all_to_all | solution.py:56
  359.0 79.0 %all-reduce = (f32[64,32]{0,1:T(8,128)S(1)}, f32[64,32]{0,1:T(8,128)S(1)}) all-reduce(f32[64,32]{0,1:T(8,128)S(1)} %convolution_bitcast_fusion.1, f32[64,32]{0,1:T(8,128)S(1)} %convolution_bitcast_fusion), channel_id=1, replica_groups=mesh['groups'=2,'rows_0'=32,'rows_1'=2,'cols'=4] {'rows_0'}, use_global_device_ids=true, to_apply=%region_10.11 | all-reduce | flops 4096 | bytes 32768 | tf_op jit(solution)/shard_map/psum | solution.py:62
  438.1 31.9 %all-reduce.2 = (f32[64,32]{0,1:T(8,128)S(1)}, f32[64,32]{0,1:T(8,128)S(1)}) all-reduce(f32[64,32]{0,1:T(8,128)S(1)} %get-tuple-element.214, f32[64,32]{0,1:T(8,128)S(1)} %get-tuple-element.215), channel_id=1, replica_groups=mesh['groups'=2,'rows_0'=32,'rows_1'=2,'cols'=4] {'rows_1'}, use_global_device_ids=true, to_apply=%region_11.12 | all-reduce | flops 4096 | bytes 32768 | tf_op jit(solution)/shard_map/psum | solution.py:62
  470.0 12.4 %all-reduce.1 = (f32[64,32]{0,1:T(8,128)}, f32[64,32]{0,1:T(8,128)}) all-reduce(f32[64,32]{0,1:T(8,128)S(1)} %get-tuple-element.218, f32[64,32]{0,1:T(8,128)S(1)} %get-tuple-element.219), channel_id=1, replica_groups=mesh['groups'=2,'rows_0'=32,'rows_1'=2,'cols'=4] {'cols'}, use_global_device_ids=true, to_apply=%region_12.13 | all-reduce | flops 4096 | bytes 32768 | tf_op jit(solution)/shard_map/psum | solution.py:62
  (92 shorter events, 63.7 us)
Async XLA Ops:
  0.6 9.7 %copy-start = (bf16[64,32]{0,1:T(8,128)(2,1)S(1)}, bf16[64,32]{0,1:T(8,128)(2,1)}, u32[]{:S(2)}) copy-start(bf16[64,32]{0,1:T(8,128)(2,1)} %param.14) | copy-start | bytes 12292
  5.2 104.9 %all-to-all-start = ((bf16[4,16,256]{2,1,0:T(8,128)(2,1)}), bf16[4,16,256]{2,1,0:T(8,128)(2,1)S(1)}, u32[]{:S(2)}, u32[]{:S(2)}) async-start(bf16[4,16,256]{2,1,0:T(8,128)(2,1)} %broadcast_in_dim.35), calls=%async_computation | async-start | bytes 65536 | tf_op jit(solution)/shard_map/all_to_all | solution.py:21
  109.2 15.6 %copy-start.1 = (bf16[1024,128]{1,0:T(8,128)(2,1)S(1)}, bf16[1024,128]{1,0:T(8,128)(2,1)}, u32[]{:S(2)}) copy-start(bf16[1024,128]{1,0:T(8,128)(2,1)} %param.15) | copy-start | bytes 786436
  109.2 15.6 %copy-start.5 = (f32[128]{0:T(128)S(1)}, f32[128]{0:T(128)}, u32[]{:S(2)}) copy-start(f32[128]{0:T(128)} %param.16) | copy-start | bytes 1540
  110.1 13.4 %all-to-all-start.1 = ((bf16[4,256,256]{2,1,0:T(8,128)(2,1)}), bf16[4,256,256]{2,1,0:T(8,128)(2,1)S(1)}, u32[]{:S(2)}, u32[]{:S(2)}) async-start(bf16[4,256,256]{2,1,0:T(8,128)(2,1)} %bitcast.6), calls=%async_computation.1 | async-start | bytes 1048576 | tf_op jit(solution)/shard_map/all_to_all | solution.py:104
  210.1 7.8 %all-to-all-start.2 = ((f32[4,16,256]{2,1,0:T(8,128)}), f32[4,16,256]{2,1,0:T(8,128)S(1)}, u32[]{:S(2)}, u32[]{:S(2)}) async-start(f32[4,16,256]{2,1,0:T(8,128)} %copy.155), calls=%async_computation.2 | async-start | bytes 131072 | tf_op jit(solution)/shard_map/all_to_all | solution.py:50
  217.8 49.4 %all-to-all-start.5 = ((bf16[64,16,128]{2,1,0:T(8,128)(2,1)}), bf16[64,16,128]{2,1,0:T(8,128)(2,1)S(1)}, u32[]{:S(2)}, u32[]{:S(2)}) async-start(bf16[64,16,128]{2,1,0:T(8,128)(2,1)} %bitcast.14), calls=%async_computation.5 | async-start | bytes 524288 | tf_op jit(solution)/shard_map/all_to_all | solution.py:56
  227.4 67.6 %copy-start.3 = (bf16[64,32]{0,1:T(8,128)(2,1)S(1)}, bf16[64,32]{0,1:T(8,128)(2,1)}, u32[]{:S(2)}) copy-start(bf16[64,32]{0,1:T(8,128)(2,1)} %param.13) | copy-start | bytes 12292
  267.2 90.7 %copy-start.2 = (f32[16,8,64]{2,1,0:T(8,128)S(1)}, f32[16,8,64]{2,1,0:T(8,128)}, u32[]{:S(2)}) copy-start(f32[16,8,64]{2,1,0:T(8,128)} %param.10) | copy-start | bytes 98308
  267.2 90.7 %copy-start.4 = (f32[64]{0:T(128)S(1)}, f32[64]{0:T(128)}, u32[]{:S(2)}) copy-start(f32[64]{0:T(128)} %param.11) | copy-start | bytes 772
  267.2 11.0 %all-to-all-start.3 = ((bf16[256,4,256]{0,2,1:T(8,128)(2,1)}), bf16[256,4,256]{0,2,1:T(8,128)(2,1)S(1)}, u32[]{:S(2)}, u32[]{:S(2)}) async-start(bf16[256,4,256]{0,2,1:T(8,128)(2,1)} %bitcast.11), calls=%async_computation.3 | async-start | bytes 1048576 | tf_op jit(solution)/shard_map/all_to_all | solution.py:155
  278.2 7.4 %all-to-all-start.6 = ((f32[4,4,128]{2,1,0:T(4,128)}), f32[4,4,128]{2,1,0:T(4,128)S(1)}, u32[]{:S(2)}, u32[]{:S(2)}) async-start(f32[4,4,128]{2,1,0:T(4,128)} %bitcast.15), calls=%async_computation.6 | async-start | bytes 16384 | tf_op jit(solution)/shard_map/all_to_all | solution.py:50
  285.6 71.9 %all-to-all-start.4 = ((bf16[64,16,256]{2,1,0:T(8,128)(2,1)}), bf16[64,16,256]{2,1,0:T(8,128)(2,1)S(1)}, u32[]{:S(2)}, u32[]{:S(2)}) async-start(bf16[64,16,256]{2,1,0:T(8,128)(2,1)} %bitcast.13), calls=%async_computation.4 | async-start | bytes 1048576 | tf_op jit(solution)/shard_map/all_to_all | solution.py:56
where the time goes:
time: 487 us; the launch traced here: 482 us
  blocking collectives  222 us (46%)
  waiting for transfers between devices  122 us (25%)
  local copies, waits for them, and re-layouts  50.5 us (10%)
  matrix products  43.3 us (9%)
  starting transfers between devices  37.3 us (8%)
  other arithmetic  6.19 us (1%)
    psum x3, blocking collectives, one_axis_at_a_time(): array = lax.psum(array, axis)  123 us
    all_to_all x2, waiting for transfers between devices, sum_at_owner(): lax.all_to_all(pieces, axis, split_axis=0, concat_axis=0, tiled=True)  102 us
    all_gather x2, blocking collectives, gather_in_order(): pieces = lax.all_gather(pieces, axes[k], axis=0, tiled=True)  98.7 us
    all_to_all x2, starting transfers between devices, sum_at_owner(): lax.all_to_all(pieces, axis, split_axis=0, concat_axis=0, tiled=True)  17.3 us
    reshape x4, local copies, waits for them, and re-layouts, advance(): outer_grad = outer_grad.reshape(step_rows, block, chans, chans)  13.3 us
    convert_element_type x4, local copies, waits for them, and re-layouts, advance(): outer_grad = jnp.dot(cot_flat, final_projector.T, preferred_element_type=...  10.3 us
    dot_general x4, matrix products, advance(): jnp.einsum('ijcd,jsd->isc', outer_grad, right_cols, preferred_element_typ...  9.97 us
  transfers between devices with their start and end apart: 7, of which 6 were waited for; matrix products, arithmetic and copies ran while one was open for 2% of the time, Pallas kernels for 0%

commit v1 on v0

v1 whole, which is shorter than its diff:
```python
import functools

import jax
import jax.numpy as jnp
from jax import lax
from jax.experimental import pallas as pl
from jax.experimental.pallas import tpu as pltpu
from jax.sharding import PartitionSpec as P

F32 = jnp.float32
BF16 = jnp.bfloat16
NEAR = 4
CORES = 2
SEMS = 96


def iota(shape, dim):
    return lax.broadcasted_iota(jnp.int32, shape, dim)


def nn(a, b):
    return jnp.dot(a, b, preferred_element_type=F32)


def nt(a, b):
    return lax.dot_general(a, b, (((1,), (1,)), ((), ())), preferred_element_type=F32)


def tn(a, b):
    return lax.dot_general(a, b, (((0,), (0,)), ((), ())), preferred_element_type=F32)


def two_part(form, a, b):
    high = a.astype(BF16)
    low = (a - high.astype(F32)).astype(BF16)
    return form(high, b) + form(low, b)


def two_part_right(form, a, b):
    high = b.astype(BF16)
    low = (b - high.astype(F32)).astype(BF16)
    return form(a, high) + form(a, low)


def kernel(
    X, Z, feat, gain, offset, p1, p2, w, bias, cot,
    out, slope, wslope, slope1, slope2,
    wf, wb, lf, lp2, lpt2, ring_r, r_all, rt, t_all, q_all,
    rb_bf, rb_own, rb_d, rb_n, rb_o, rb_r, rb_x, rb_q, ru_s, ru_r, rd_s, rd_r,
    lb_acc, lb, lb_r, s_all, s_d, s_x, s_xr, s_n, s_nr, s_g, s_row,
    v_s, v_rs, v_n, v_nr, v_g, v_f, send_sem, recv_sem,
):
    ring = Z // NEAR
    mem = Z // X // NEAR
    tok = feat.shape[0]
    pairs = tok // 2
    s8 = feat.shape[1]
    width = w.shape[0] // p1.shape[1]
    lanes = width * s8
    xi = lax.axis_index("cols")
    row = lax.axis_index("rows")
    z, core = row // CORES, row % CORES
    a, m = z % NEAR, z // NEAR
    scale = 1.0 / (s8 * X)

    def at(dx=0, dz=0, other=None):
        k = core if other is None else other
        return {"rows": ((z + dz + Z) % Z) * CORES + k, "cols": (xi + dx) % X}

    used = [0]

    def send(src, dst, device):
        k = used[0]
        used[0] += 1
        copy = pltpu.make_async_remote_copy(
            src_ref=src, dst_ref=dst, send_sem=send_sem.at[k], recv_sem=recv_sem.at[k],
            device_id=device, device_id_type=pl.DeviceIdType.MESH,
        )
        copy.start()
        return copy

    started = []

    def go(src, dst, device):
        copy = send(src, dst, device)
        started.append(copy)
        return copy

    level = CORES * X
    here = xi * CORES + core

    def peer(o):
        there = (here + o) % level
        return there, {"rows": z * CORES + there % CORES, "cols": there // CORES}

    steps = (1, -1, 2, -2, NEAR, -NEAR)
    barrier = pltpu.get_barrier_semaphore()
    for o in range(1, level):
        pl.semaphore_signal(barrier, inc=1, device_id=peer(o)[1], device_id_type=pl.DeviceIdType.MESH)
    for dz in steps:
        pl.semaphore_signal(barrier, inc=1, device_id=at(dz=dz), device_id_type=pl.DeviceIdType.MESH)

    f = feat[...]
    centred = f - jnp.mean(f, axis=-1, keepdims=True)
    rs = lax.rsqrt(jnp.mean(centred * centred, axis=-1, keepdims=True) + 1e-05)
    xhat = centred * rs
    normed = xhat * gain[...][None] + offset[...][None]
    depth = f.shape[2]
    split = normed.reshape(pairs, 2, s8, depth)
    even = split[:, 0].reshape(pairs * s8, depth).astype(BF16)
    odd = split[:, 1].reshape(pairs * s8, depth).astype(BF16)
    nb = normed.reshape(tok * s8, depth).astype(BF16)

    rep = (iota((width, lanes), 1) // s8 == iota((width, lanes), 0)).astype(BF16)
    p2r = nn(p2[...], rep).astype(BF16)
    half = 2 * 2 * width
    col = iota((width, half), 1)
    same = col % width == iota((width, half), 0)
    p1e = nn(p1[...], (same & ((col // width) % 2 == 0)).astype(BF16)).astype(BF16)
    p1o = nn(p1[...], (same & ((col // width) % 2 == 1)).astype(BF16)).astype(BF16)
    pick = iota((tok, s8, lanes), 1) == iota((tok, s8, lanes), 2) % s8

    right = nn(nb, p2r).reshape(tok, s8, lanes)
    ring_r[m] = jnp.sum(jnp.where(pick, right, 0.0), axis=1).astype(BF16)
    left = (nn(even, p1e) + nn(odd, p1o)).astype(BF16).astype(F32)
    lf[:, xi] = left.reshape(pairs, s8, half)

    wf[...] = w[...].astype(F32)
    wb[...] = jnp.zeros_like(wb)

    def spread(g, _):
        for d2 in range(2):
            piece = wf[pl.ds(2 * g + d2, width, stride=width), :].astype(BF16)
            for i in range(2):
                at_row = (d2 * 2 + i) * width
                wb[g, at_row : at_row + width, i * 128 : (i + 1) * 128] = piece
        return 0

    lax.fori_loop(0, width // 2, spread, 0)
    pl.semaphore_wait(barrier, level - 1 + len(steps))

    def ring_up(buf, t):
        q = (m - t + 1 + ring) % ring
        return go(buf.at[q], buf.at[q], at(dz=NEAR))

    def ring_down(buf, t):
        q = (m + t - 1) % ring
        return go(buf.at[q], buf.at[q], at(dz=-NEAR))

    ups, downs = ring // 2, ring // 2 - 1

    lefts = [go(lf.at[:, xi], lf.at[:, xi], at(dx=dx)) for dx in range(1, X)]
    up, down = ring_up(ring_r, 1), ring_down(ring_r, 1)
    for copy in lefts:
        copy.wait_recv()

    lane = iota((pairs * X, s8, half), 2)
    lfull = lf[...].reshape(pairs * X, s8, half)
    zero = jnp.zeros_like(lfull)
    both = jnp.concatenate(
        [jnp.where(lane < half // 2, lfull, zero), jnp.where(lane >= half // 2, lfull, zero)], axis=1
    )
    lp2[...] = both.reshape(pairs * X * s8 * 2, half).astype(BF16)
    er, ec = iota((half, half), 0), iota((half, half), 1)
    kept = (er // width) * width + (er % ring) * NEAR + (er % width) // ring
    lpt2[...] = nt((kept == ec).astype(BF16), lp2[...]).astype(BF16)

    def make_t(g, _):
        piece = nn(lp2[...], wb[g]).astype(BF16).reshape(pairs, X, 2 * s8, 256)
        t_all[:, :, pl.ds(pl.multiple_of(g * 2 * s8, 2 * s8), 2 * s8), :] = piece
        return 0

    lax.fori_loop(0, width // 2, make_t, 0)

    up.wait_recv()
    up2 = ring_up(ring_r, 2)
    down.wait_recv()
    down2 = ring_down(ring_r, 2)

    def pair_of(p):
        return jnp.concatenate([cot[2 * p], cot[2 * p + 1]], axis=-1)

    def make_rb(k, _):
        total = nt(pair_of(0), t_all[0, k])
        for p in range(1, pairs):
            total = total + nt(pair_of(p), t_all[p, k])
        total = (total * scale).reshape(mem, NEAR, CORES, tok, lanes)
        rb_bf[k] = total.astype(BF16)
        rb_own[k] = total
        return 0

    lax.fori_loop(0, X, make_rb, 0)
    rbd = go(rb_bf.at[:, :, :, 1 - core], rb_d, at(other=1 - core))

    up2.wait_recv()
    up3 = ring_up(ring_r, 3)
    down2.wait_recv()
    down3 = ring_down(ring_r, 3)

    rbd.wait_recv()
    for k in range(NEAR):
        piece = rb_own[:, :, k, core] + rb_d[:, :, k].astype(F32)
        rb_n[k] = piece.astype(BF16)
    rb_o[...] = rb_own[:, :, a, core] + rb_d[:, :, a].astype(F32)
    hx = X // 2
    rbn = [
        go(rb_n.at[(a + 1) % NEAR], rb_r.at[0], at(dz=1)),
        go(rb_n.at[(a + 3) % NEAR], rb_r.at[1], at(dz=-1)),
        go(rb_n.at[(a + 2) % NEAR, 0:hx], rb_r.at[2, 0:hx], at(dz=2)),
        go(rb_n.at[(a + 2) % NEAR, hx:X], rb_r.at[2, hx:X], at(dz=-2)),
    ]

    up3.wait_recv()
    up4 = ring_up(ring_r, 4)

    for copy in rbn:
        copy.wait_recv()
    rb_x[...] = (
        rb_o[...] + rb_r[0].astype(F32) + rb_r[1].astype(F32) + rb_r[2].astype(F32)
    ).astype(BF16)
    rb_q[pl.ds(xi * mem, mem)] = rb_x[xi]
    rbx = [
        go(rb_x.at[(xi + dx) % X], rb_q.at[pl.ds(xi * mem, mem)], at(dx=dx)) for dx in range(1, X)
    ]

    up4.wait_recv()
    down3.wait_recv()
    r_all[xi, :, a, core] = ring_r[pl.ds(xi * mem, mem)]
    rx = [
        go(ring_r.at[pl.ds(((xi + dx) % X) * mem, mem)], r_all.at[xi, :, a, core], at(dx=dx))
        for dx in range(1, X)
    ]

    for copy in rbx:
        copy.wait_recv()

    def rb_up(t):
        q = (m + ups + 1 - t) % ring
        value = rb_q[q].astype(F32)
        if t > 1:
            value = value + ru_r[t - 2].astype(F32)
        ru_s[t - 1] = value.astype(BF16)
        return go(ru_s.at[t - 1], ru_r.at[t - 1], at(dz=NEAR))

    def rb_down(t):
        q = (m - downs - 1 + t + ring) % ring
        value = rb_q[q].astype(F32)
        if t > 1:
            value = value + rd_r[t - 2].astype(F32)
        rd_s[t - 1] = value.astype(BF16)
        return go(rd_s.at[t - 1], rd_r.at[t - 1], at(dz=-NEAR))

    bu, bd = rb_up(1), rb_down(1)

    for copy in rx:
        copy.wait_recv()
    rn = [
        go(r_all.at[:, :, a, core], r_all.at[:, :, a, core], at(dz=1)),
        go(r_all.at[:, :, a, core], r_all.at[:, :, a, core], at(dz=-1)),
        go(r_all.at[0:hx, :, a, core], r_all.at[0:hx, :, a, core], at(dz=2)),
        go(r_all.at[hx:X, :, a, core], r_all.at[hx:X, :, a, core], at(dz=-2)),
    ]
    partner = at(other=1 - core)

    def to_partner(k):
        return go(r_all.at[:, :, k, core], r_all.at[:, :, k, core], partner)

    cores = [to_partner(a)]

    bu.wait_recv()
    bu = rb_up(2)
    bd.wait_recv()
    bd = rb_down(2)

    rn[0].wait_recv()
    cores.append(to_partner((a + 3) % NEAR))
    rn[1].wait_recv()
    cores.append(to_partner((a + 1) % NEAR))
    rn[2].wait_recv()
    rn[3].wait_recv()
    cores.append(to_partner((a + 2) % NEAR))
    for copy in cores:
        copy.wait_recv()

    block = mem * NEAR * CORES * tok

    def turn(k, _):
        rt[k] = r_all[k].reshape(block, lanes).T
        return 0

    lax.fori_loop(0, X, turn, 0)

    def make_q(p, _):
        pair = pair_of(p)
        for k in range(X):
            q_all[p, k] = nn(rt[k], pair).astype(BF16)
        return 0

    lax.fori_loop(0, pairs, make_q, 0)

    lb_acc[...] = jnp.zeros_like(lb_acc)

    def make_s(g, _):
        for u in range(2):
            at_row = pl.multiple_of((2 * g + u) * 2 * s8, 2 * s8)
            piece = q_all[:, :, pl.ds(at_row, 2 * s8), :].reshape(pairs * X * 2 * s8, 256)
            lb_acc[...] += nt(piece, wb[2 * g + u])
            found = nn(lpt2[...], piece) * scale
            for d2 in range(2):
                top = d2 * 2 * width
                s_all[g, :, (2 * u + d2) * 128 : (2 * u + d2 + 1) * 128] = (
                    found[top : top + width, 0:128] + found[top + width : top + 2 * width, 128:256]
                )
        return 0

    lax.fori_loop(0, width // 4, make_s, 0)
    sd = go(s_all.at[pl.ds((1 - core) * X, X)], s_d, partner)
    acc = lb_acc[...].reshape(pairs * X, 2, s8, half)
    lb[...] = (jnp.where(lane < half // 2, acc[:, 0], acc[:, 1]) * scale).reshape(pairs, X, s8, half)
    lbx = [go(lb.at[:, (xi + dx) % X], lb_r.at[dx - 1], at(dx=dx)) for dx in range(1, X)]

    bu.wait_recv()
    bu = rb_up(3)
    bd.wait_recv()
    bd = rb_down(3)

    sd.wait_recv()
    s_x[...] = (s_all[pl.ds(core * X, X)] + s_d[...]).astype(BF16)
    sx = [go(s_x.at[(xi + dx) % X], s_xr.at[dx - 1], at(dx=dx)) for dx in range(1, X)]

    def make_update(p, _):
        total = nn(r_all[0].reshape(block, lanes), t_all[p, 0])
        for k in range(1, X):
            total = total + nn(r_all[k].reshape(block, lanes), t_all[p, k])
        total = total * scale
        out[2 * p] = (total[:, 0:128] + bias[...]).astype(BF16)
        out[2 * p + 1] = (total[:, 128:256] + bias[...]).astype(BF16)
        return 0

    lax.fori_loop(0, pairs // 2, make_update, 0)

    for copy in lbx:
        copy.wait_recv()
    lsum = (lb[:, xi] + lb_r[0] + lb_r[1] + lb_r[2]).reshape(pairs * s8, half)

    for copy in sx:
        copy.wait_recv()
    stot = s_x[xi].astype(F32)
    for k in range(X - 1):
        stot = stot + s_xr[k].astype(F32)
    s_n[...] = stot.reshape(NEAR, ring, stot.shape[1])
    sn = [
        go(s_n.at[(a + 1) % NEAR], s_nr.at[0], at(dz=1)),
        go(s_n.at[(a + 3) % NEAR], s_nr.at[1], at(dz=-1)),
        go(s_n.at[(a + 2) % NEAR], s_nr.at[2], at(dz=2)),
    ]

    bu.wait_recv()
    bu = rb_up(4)
    lax.fori_loop(pairs // 2, pairs, make_update, 0)

    for copy in sn:
        copy.wait_recv()
    tile = s_n[a] + s_nr[0] + s_nr[1] + s_nr[2]
    s_g[m] = jnp.concatenate([tile[:, 0:256], tile[:, 256:512]], axis=0).astype(BF16)
    su, sdn = ring_up(s_g, 1), ring_down(s_g, 1)

    bu.wait_recv()
    bd.wait_recv()
    rb = rb_q[m].astype(F32) + ru_r[ups - 1].astype(F32) + rd_r[downs - 1].astype(F32)
    wide = jnp.where(pick, rb.reshape(tok, 1, lanes), 0.0).reshape(tok * s8, lanes)

    f1 = two_part_right(tn, even, lsum)
    f2 = two_part_right(tn, odd, lsum)
    ftot = jnp.where((iota(f1.shape, 1) // width) % 2 == 0, f1, f2)
    fold1 = (er % width == ec).astype(BF16)
    g2 = two_part_right(tn, nb, wide)
    fold2 = (iota((lanes, half), 0) // s8 + width == iota((lanes, half), 1)).astype(BF16)
    vtot = two_part(nn, ftot, fold1) + two_part(nn, g2, fold2)
    v_s[...] = vtot.reshape(level, depth // level, half)
    vrs = []
    for o in range(1, level):
        there, device = peer(o)
        vrs.append(go(v_s.at[there], v_rs.at[o - 1], device))

    from_right = two_part(nt, wide, p2r)
    from_even = two_part(nt, lsum, p1e).reshape(pairs, 1, s8, depth)
    from_odd = two_part(nt, lsum, p1o).reshape(pairs, 1, s8, depth)
    from_left = jnp.concatenate([from_even, from_odd], axis=1).reshape(tok, s8, depth)
    scaled = (from_right.reshape(tok, s8, depth) + from_left) * gain[...][None]
    slope[...] = rs * (
        scaled
        - jnp.mean(scaled, axis=-1, keepdims=True)
        - xhat * jnp.mean(scaled * xhat, axis=-1, keepdims=True)
    )

    for copy in vrs:
        copy.wait_recv()
    vsum = v_s[here]
    for k in range(level - 1):
        vsum = vsum + v_rs[k]
    v_n[...] = vsum
    vn = [go(v_n, v_nr.at[k], at(dz=dz)) for k, dz in enumerate((1, -1, 2))]
    su.wait_recv()
    su = ring_up(s_g, 2)
    sdn.wait_recv()
    sdn = ring_down(s_g, 2)
    for copy in vn:
        copy.wait_recv()
    v_g[m] = v_n[...] + v_nr[0] + v_nr[1] + v_nr[2]
    vu, vd = ring_up(v_g, 1), ring_down(v_g, 1)
    for t in range(3, ups + 1):
        su.wait_recv()
        su = ring_up(s_g, t)
        if t <= downs:
            sdn.wait_recv()
            sdn = ring_down(s_g, t)
        vu.wait_recv()
        vu = ring_up(v_g, t - 1)
        vd.wait_recv()
        vd = ring_down(v_g, t - 1) if t - 1 <= downs else None
    su.wait_recv()
    if downs > 2:
        sdn.wait_recv()
    vu.wait_recv()
    vu = ring_up(v_g, ups)
    stile = s_g[0].astype(F32)
    for k in range(1, ring):
        stile = stile + s_g[k].astype(F32)
    s_row[...] = stile
    for h in range(2):
        line = s_row[pl.ds(m + h * ring, 1), :]
        wslope[2 * h : 2 * h + 1, :] = line[:, 0:128]
        wslope[2 * h + 1 : 2 * h + 2, :] = line[:, 128:256]
    vu.wait_recv()
    if vd is not None:
        vd.wait_recv()
    vtile = v_g[0]
    for k in range(1, ring):
        vtile = vtile + v_g[k]
    v_f[here] = vtile
    vag = [go(v_f.at[here], v_f.at[here], peer(o)[1]) for o in range(1, level)]
    for copy in vag:
        copy.wait_recv()
    vfull = v_f[...].reshape(depth, half)
    slope1[...] = vfull[:, 0:width]
    slope2[...] = vfull[:, width : 2 * width]

    for copy in started:
        copy.wait_send()


def solution(mesh):
    X, Z = mesh.shape["cols"], mesh.shape["rows"] // CORES

    def local(feat, gain, offset, p1, p2, w, bias, cot):
        tok, s8, depth = feat.shape
        width = p1.shape[1]
        pair_ch = w.shape[1]
        block = cot.shape[1]
        ring, mem, pairs = Z // NEAR, Z // X // NEAR, tok // 2
        lanes, half, seqs = width * s8, 4 * width, s8 * X
        level = CORES * X
        v = pltpu.VMEM
        scratch = [
            v(w.shape, F32),
            v((width // 2, half, 2 * pair_ch), BF16),
            v((pairs, X, s8, half), F32),
            v((pairs * seqs * 2, half), BF16),
            v((half, pairs * seqs * 2), BF16),
            v((ring, tok, lanes), BF16),
            v((X, mem, NEAR, CORES, tok, lanes), BF16),
            v((X, lanes, block), BF16),
            v((pairs, X, lanes, 2 * pair_ch), BF16),
            v((pairs, X, lanes, 2 * pair_ch), BF16),
            v((X, mem, NEAR, CORES, tok, lanes), BF16),
            v((X, mem, NEAR, CORES, tok, lanes), F32),
            v((X, mem, NEAR, tok, lanes), BF16),
            v((NEAR, X, mem, tok, lanes), BF16),
            v((X, mem, tok, lanes), F32),
            v((NEAR - 1, X, mem, tok, lanes), BF16),
            v((X, mem, tok, lanes), BF16),
            v((ring, tok, lanes), BF16),
            v((ring // 2, tok, lanes), BF16),
            v((ring // 2, tok, lanes), BF16),
            v((ring // 2, tok, lanes), BF16),
            v((ring // 2, tok, lanes), BF16),
            v((pairs * seqs * 2, half), F32),
            v((pairs, X, s8, half), F32),
            v((X - 1, pairs, s8, half), F32),
            v((CORES * X, width, width // level * pair_ch), F32),
            v((X, width, width // level * pair_ch), F32),
            v((X, width, width // level * pair_ch), BF16),
            v((X - 1, width, width // level * pair_ch), BF16),
            v((NEAR, ring, width // level * pair_ch), F32),
            v((NEAR - 1, ring, width // level * pair_ch), F32),
            v((ring, 2 * ring, 2 * pair_ch), BF16),
            v((2 * ring, 2 * pair_ch), F32),
            v((level, depth // level, half), F32),
            v((level - 1, depth // level, half), F32),
            v((depth // level, half), F32),
            v((NEAR - 1, depth // level, half), F32),
            v((ring, depth // level, half), F32),
            v((level, depth // level, half), F32),
            pltpu.SemaphoreType.DMA((SEMS,)),
            pltpu.SemaphoreType.DMA((SEMS,)),
        ]
        whole = pl.BlockSpec(memory_space=pltpu.VMEM)
        shape = jax.ShapeDtypeStruct
        return pl.pallas_call(
            functools.partial(kernel, X, Z),
            out_shape=(
                shape(cot.shape, BF16),
                shape(feat.shape, F32),
                shape((w.shape[0] // (Z * level), pair_ch), F32),
                shape((depth, width), F32),
                shape((depth, width), F32),
            ),
            in_specs=[whole] * 8,
            out_specs=(whole,) * 5,
            scratch_shapes=scratch,
            compiler_params=pltpu.CompilerParams(collective_id=0, has_side_effects=True),
            name="outer_mean",
        )(feat, gain.reshape(1, -1), offset.reshape(1, -1), p1, p2, w, bias.reshape(1, -1), cot)

    tokens = P(("groups", "rows"), "cols", None)
    return jax.shard_map(
        local,
        mesh=mesh,
        in_specs=(tokens, P(), P(), P(), P(), P(), P(), tokens),
        out_specs=(tokens, tokens, P(("groups", "rows", "cols"), None), P("groups", None), P("groups", None)),
        check_vma=False,
    )
```

time: 487 us -> 136 us (0.28)
  blocking collectives: 222 us -> 0 us
  Pallas kernels: 0 us -> 128 us
  waiting for transfers between devices: 122 us -> 0 us
  matrix products: 43.3 us -> 0 us
  local copies, waits for them, and re-layouts: 50.5 us -> 7.8 us
  starting transfers between devices: 37.3 us -> 0 us
  other arithmetic: 6.19 us -> 0 us
    pallas_call x0 -> x1, Pallas kernels: none -> 128 us  [local(): pl.pallas_call(functools.partial(kernel, X, Z), out_shape=(shape(cot.shap...]
    psum x3 -> x0, blocking collectives: 123 us -> none  [one_axis_at_a_time(): array = lax.psum(array, axis)]
    all_to_all x7 -> x0, waiting for transfers between devices: 122 us -> none  [the longest x2 102 us: sum_at_owner(): lax.all_to_all(pieces, axis, split_axis=0, concat_axis=0, tiled=True)]
    all_gather x2 -> x0, blocking collectives: 98.7 us -> none  [gather_in_order(): pieces = lax.all_gather(pieces, axes[k], axis=0, tiled=True)]
    dot_general x30 -> x0, matrix products: 43.3 us -> none  [the longest x4 9.97 us: advance(): jnp.einsum('ijcd,jsd->isc', outer_grad, right_cols, preferred_element_typ...]
    all_to_all x7 -> x0, starting transfers between devices: 37.3 us -> none  [the longest x2 17.3 us: sum_at_owner(): lax.all_to_all(pieces, axis, split_axis=0, concat_axis=0, tiled=True)]
    convert_element_type x10 -> x0, local copies, waits for them, and re-layouts: 16.8 us -> none  [the longest x4 10.3 us: advance(): outer_grad = jnp.dot(cot_flat, final_projector.T, preferred_element_type=...]
    reshape x7 -> x0, local copies, waits for them, and re-layouts: 13.6 us -> none  [the longest x4 13.3 us: advance(): outer_grad = outer_grad.reshape(step_rows, block, chans, chans)]
  transfers between devices with their start and end apart: 7 -> 0, of which waited for: 6 -> 0; matrix products, arithmetic and copies ran while one was open for 2% -> 0% of each run, Pallas kernels for 0% -> 0%
where the time goes in v1:
time: 136 us
  Pallas kernels  128 us (94%)
  local copies, waits for them, and re-layouts  7.8 us (6%)
    pallas_call x1, Pallas kernels, local(): pl.pallas_call(functools.partial(kernel, X, Z), out_shape=(shape(cot.shap...  128 us
    unnamed x13, local copies, waits for them, and re-layouts  5.67 us

profile of v1, /device:TPU:33, one launch (start us, length us, event | category | flops | bytes accessed | tf_op | source)
XLA Modules:
  0.0 136.2 jit_solution(1457977769500796151)
XLA Ops:
  0.6 0.0 copy-start.2
  0.6 1.4 %copy.13.p1 = bf16[64,32]{1,0:T(8,128)(2,1)} copy(bf16[64,32]{0,1:T(8,128)(2,1)} %param.11) | data formatting | bytes 8192 | tf_op args[3]
  2.0 0.0 copy-done.2
  2.0 0.7 copy.14.p2
  2.7 127.7 %outer_mean.1 = (bf16[16,256,128]{2,1,0:T(8,128)(2,1)}, f32[16,8,64]{2,1,0:T(8,128)}, f32[4,128]{1,0:T(4,128)}, f32[64,32]{1,0:T(8,128)}, f32[64,32]{1,0:T(8,128)}) custom-call(f32[16,8,64]{2,1,0:T(8,128)} %feat.1, f32[1,64]{1,0:T(1,128)} %bitcast.3, f32[1,64]{1,0:T(1,128)} %bitcast.4, bf16[64,32]{1,0:T(8,128)(2,1)} %copy.13.p1, bf16[64,32]{1,0:T(8,128)(2,1)} %copy.14.p2, ...), custom_call_target="tpu_custom_call" | custom-call | tf_op jit(solution)/shard_map/outer_mean/pallas_call | solution.py:510
  130.4 0.0 copy-start.1
  130.5 1.4 %copy.15 = f32[64,32]{0,1:T(8,128)} copy(f32[64,32]{1,0:T(8,128)} %get-tuple-element.8) | data formatting | bytes 16384 | tf_op jit(solution)/shard_map/outer_mean/pallas_call | solution.py:510
  131.9 0.0 copy-done.1
  131.9 0.7 copy.16
  132.6 0.0 copy-start
  132.6 2.3 %copy.20 = bf16[16,256,128]{2,1,0:T(8,128)(2,1)} copy(bf16[16,256,128]{2,1,0:T(8,128)(2,1)} %get-tuple-element.15) | data formatting | bytes 2097152
  134.9 0.0 copy-done
  134.9 0.0 copy-start.3
  134.9 0.6 copy.21
  135.5 0.0 copy-done.3
  135.6 0.6 copy.22
Async XLA Ops:
  0.6 1.4 %copy-start.2 = (bf16[64,32]{0,1:T(8,128)(2,1)S(1)}, bf16[64,32]{0,1:T(8,128)(2,1)}, u32[]{:S(2)}) copy-start(bf16[64,32]{0,1:T(8,128)(2,1)} %param.12) | copy-start | bytes 12292
  130.4 1.5 %copy-start.1 = (f32[64,32]{1,0:T(8,128)S(1)}, f32[64,32]{1,0:T(8,128)}, u32[]{:S(2)}) copy-start(f32[64,32]{1,0:T(8,128)} %get-tuple-element.9) | copy-start | bytes 24580
  132.6 2.3 %copy-start = (f32[16,8,64]{2,1,0:T(8,128)S(1)}, f32[16,8,64]{2,1,0:T(8,128)}, u32[]{:S(2)}) copy-start(f32[16,8,64]{2,1,0:T(8,128)} %get-tuple-element.16) | copy-start | bytes 98308
  134.9 0.7 copy-start.3

commit v2 on v1

v2 whole, which is shorter than its diff:
```python
import functools

import jax
import jax.numpy as jnp
from jax import lax
from jax.experimental import pallas as pl
from jax.experimental.pallas import tpu as pltpu
from jax.sharding import PartitionSpec as P

F32 = jnp.float32
BF16 = jnp.bfloat16
NEAR = 4
CORES = 2
SEMS = 96
VMEM_BYTES = 66 * 1000 * 1000


def iota(shape, dim):
    return lax.broadcasted_iota(jnp.int32, shape, dim)


def nn(a, b):
    return jnp.dot(a, b, preferred_element_type=F32)


def nt(a, b):
    return lax.dot_general(a, b, (((1,), (1,)), ((), ())), preferred_element_type=F32)


def tn(a, b):
    return lax.dot_general(a, b, (((0,), (0,)), ((), ())), preferred_element_type=F32)


def two_part(form, a, b):
    high = a.astype(BF16)
    low = (a - high.astype(F32)).astype(BF16)
    return form(high, b) + form(low, b)


def kernel(
    X, Z, feat_in, gain_in, offset_in, p1_in, p2_in, w_in, bias_in, cot_in,
    out_away, slope, wslope, slope1, slope2,
    out, feat, gain, offset, p1, p2, w, bias, cot, wf, wb, lf, lp2, lpt2, ring_r, r_all, rt, t_all, q_all,
    rb_bf, rb_own, rb_d, rb_n, rb_o, rb_r, rb_x, rb_q, rb_f,
    lb_acc, lb, lb_r, s_all, s_rs, s_n, s_nr, s_f, s_fr,
    v_s, v_rs, v_n, v_nr, v_t, v_fr, v_f, send_sem, recv_sem, load_sem,
):
    ring = Z // NEAR
    mem = Z // X // NEAR
    tok = feat.shape[0]
    pairs = tok // 2
    s8 = feat.shape[1]
    width = p1.shape[0]
    lanes = width * s8
    xi = lax.axis_index("cols")
    row = lax.axis_index("rows")
    z, core = row // CORES, row % CORES
    a, m = z % NEAR, z // NEAR
    scale = 1.0 / (s8 * X)

    def at(dx=0, dz=0, other=None):
        k = core if other is None else other
        return {"rows": ((z + dz + Z) % Z) * CORES + k, "cols": (xi + dx) % X}

    used = [0]

    def send(src, dst, device):
        k = used[0]
        used[0] += 1
        copy = pltpu.make_async_remote_copy(
            src_ref=src, dst_ref=dst, send_sem=send_sem.at[k], recv_sem=recv_sem.at[k],
            device_id=device, device_id_type=pl.DeviceIdType.MESH,
        )
        copy.start()
        return copy

    started = []

    def go(src, dst, device):
        copy = send(src, dst, device)
        started.append(copy)
        return copy

    level = CORES * X
    here = xi * CORES + core

    def peer(o):
        there = (here + o) % level
        return there, {"rows": z * CORES + there % CORES, "cols": there // CORES}

    sources = (feat_in, gain_in, offset_in, p2_in, p1_in, w_in, bias_in, cot_in)
    targets = (feat, gain, offset, p2, p1, w, bias, cot)
    loads = [
        pltpu.make_async_copy(source, target, load_sem.at[k])
        for k, (source, target) in enumerate(zip(sources, targets))
    ]
    for copy in loads:
        copy.start()
    steps = (1, -1, 2, -2, NEAR, -NEAR)
    barrier = pltpu.get_barrier_semaphore()
    for o in range(1, level):
        pl.semaphore_signal(barrier, inc=1, device_id=peer(o)[1], device_id_type=pl.DeviceIdType.MESH)
    for dz in steps:
        pl.semaphore_signal(barrier, inc=1, device_id=at(dz=dz), device_id_type=pl.DeviceIdType.MESH)

    for copy in loads[:5]:
        copy.wait()
    f = feat[...]
    centred = f - jnp.mean(f, axis=-1, keepdims=True)
    rs = lax.rsqrt(jnp.mean(centred * centred, axis=-1, keepdims=True) + 1e-05)
    xhat = centred * rs
    normed = xhat * gain[...][None] + offset[...][None]
    depth = f.shape[2]
    split = normed.reshape(pairs, 2, s8, depth)
    even = split[:, 0].reshape(pairs * s8, depth).astype(BF16)
    odd = split[:, 1].reshape(pairs * s8, depth).astype(BF16)
    nb = normed.reshape(tok * s8, depth).astype(BF16)

    rep = (iota((width, lanes), 1) // s8 == iota((width, lanes), 0)).astype(BF16)
    p2r = tn(p2[...], rep).astype(BF16)
    half = 2 * 2 * width
    col = iota((width, half), 1)
    same = col % width == iota((width, half), 0)
    p1e = tn(p1[...], (same & ((col // width) % 2 == 0)).astype(BF16)).astype(BF16)
    p1o = tn(p1[...], (same & ((col // width) % 2 == 1)).astype(BF16)).astype(BF16)
    pick = iota((tok, s8, lanes), 1) == iota((tok, s8, lanes), 2) % s8

    right = nn(nb, p2r).reshape(tok, s8, lanes)
    ring_r[m] = jnp.sum(jnp.where(pick, right, 0.0), axis=1).astype(BF16)
    left = (nn(even, p1e) + nn(odd, p1o)).astype(BF16).astype(F32)
    lf[:, xi] = left.reshape(pairs, s8, half)

    wb[...] = jnp.zeros_like(wb)
    loads[5].wait()
    wf[...] = w[...].astype(F32)

    def spread(g, _):
        for d2 in range(2):
            piece = wf[pl.ds(2 * g + d2, width, stride=width), :].astype(BF16)
            for i in range(2):
                at_row = (d2 * 2 + i) * width
                wb[g, at_row : at_row + width, i * 128 : (i + 1) * 128] = piece
        return 0

    lax.fori_loop(0, width // 2, spread, 0)
    pl.semaphore_wait(barrier, level - 1 + len(steps))

    def ring_up(buf, t):
        q = (m - t + 1 + ring) % ring
        return go(buf.at[q], buf.at[q], at(dz=NEAR))

    def ring_down(buf, t):
        q = (m + t - 1) % ring
        return go(buf.at[q], buf.at[q], at(dz=-NEAR))

    ups, downs = ring // 2, ring // 2 - 1

    lefts = [go(lf.at[:, xi], lf.at[:, xi], at(dx=dx)) for dx in range(1, X)]
    up, down = ring_up(ring_r, 1), ring_down(ring_r, 1)
    for copy in lefts:
        copy.wait_recv()

    lane = iota((pairs * X, s8, half), 2)
    lfull = lf[...].reshape(pairs * X, s8, half)
    zero = jnp.zeros_like(lfull)
    both = jnp.concatenate(
        [jnp.where(lane < half // 2, lfull, zero), jnp.where(lane >= half // 2, lfull, zero)], axis=1
    )
    lp2[...] = both.reshape(pairs * X * s8 * 2, half).astype(BF16)
    er, ec = iota((half, half), 0), iota((half, half), 1)
    kept = (er // width) * width + (er % ring) * NEAR + (er % width) // ring
    lpt2[...] = nt((kept == ec).astype(BF16), lp2[...]).astype(BF16)

    def make_t(g, _):
        for u in range(2):
            piece = nn(lp2[...], wb[2 * g + u]).astype(BF16).reshape(pairs, X, 2 * s8, 256)
            at_row = pl.multiple_of((2 * g + u) * 2 * s8, 2 * s8)
            t_all[:, :, pl.ds(at_row, 2 * s8), :] = piece
        return 0

    lax.fori_loop(0, width // 8, make_t, 0)

    up.wait_recv()
    up2 = ring_up(ring_r, 2)
    down.wait_recv()
    down2 = ring_down(ring_r, 2)
    lax.fori_loop(width // 8, width // 4, make_t, 0)
    loads[6].wait()
    loads[7].wait()

    def pair_of(p):
        return jnp.concatenate([cot[2 * p], cot[2 * p + 1]], axis=-1)

    def make_rb(k, _):
        total = nt(pair_of(0), t_all[0, k])
        for p in range(1, pairs):
            total = total + nt(pair_of(p), t_all[p, k])
        total = (total * scale).reshape(mem, NEAR, CORES, tok, lanes)
        rb_bf[k] = total.astype(BF16)
        rb_own[k] = total
        return 0

    lax.fori_loop(0, X, make_rb, 0)
    rbd = go(rb_bf.at[:, :, :, 1 - core], rb_d, at(other=1 - core))

    up2.wait_recv()
    up3 = ring_up(ring_r, 3)
    down2.wait_recv()
    down3 = ring_down(ring_r, 3)

    rbd.wait_recv()
    for k in range(NEAR):
        piece = rb_own[:, :, k, core] + rb_d[:, :, k].astype(F32)
        rb_n[k] = piece.astype(BF16)
    hx = X // 2
    rbn = [
        go(rb_n.at[(a + 1) % NEAR], rb_r.at[0], at(dz=1)),
        go(rb_n.at[(a + 3) % NEAR], rb_r.at[1], at(dz=-1)),
        go(rb_n.at[(a + 2) % NEAR, 0:hx], rb_r.at[2, 0:hx], at(dz=2)),
        go(rb_n.at[(a + 2) % NEAR, hx:X], rb_r.at[2, hx:X], at(dz=-2)),
    ]
    rb_o[...] = rb_own[:, :, a, core] + rb_d[:, :, a].astype(F32)

    up3.wait_recv()
    up4 = ring_up(ring_r, 4)

    for copy in rbn:
        copy.wait_recv()
    rb_x[...] = (
        rb_o[...] + rb_r[0].astype(F32) + rb_r[1].astype(F32) + rb_r[2].astype(F32)
    ).astype(BF16)
    rbx = [
        go(rb_x.at[(xi + dx) % X], rb_q.at[pl.ds(xi * mem, mem)], at(dx=dx)) for dx in range(1, X)
    ]
    rb_q[pl.ds(xi * mem, mem)] = rb_x[xi]

    down3.wait_recv()
    up4.wait_recv()
    rx = [
        go(ring_r.at[pl.ds(((xi + dx) % X) * mem, mem)], r_all.at[xi, :, a, core], at(dx=dx))
        for dx in range(1, X)
    ]
    r_all[xi, :, a, core] = ring_r[pl.ds(xi * mem, mem)]
    partner = at(other=1 - core)

    for copy in rx:
        copy.wait_recv()
    rn = [
        go(r_all.at[:, :, a, core], r_all.at[:, :, a, core], at(dz=1)),
        go(r_all.at[:, :, a, core], r_all.at[:, :, a, core], at(dz=-1)),
        go(r_all.at[0:hx, :, a, core], r_all.at[0:hx, :, a, core], at(dz=2)),
        go(r_all.at[hx:X, :, a, core], r_all.at[hx:X, :, a, core], at(dz=-2)),
    ]

    def to_partner(k):
        return go(r_all.at[:, :, k, core], r_all.at[:, :, k, core], partner)

    cores = [to_partner(a)]

    def far(o):
        return (m + o) % ring, at(dz=NEAR * o)

    for copy in rbx:
        copy.wait_recv()
    rbf = []
    for o in range(1, ring):
        there, device = far(o)
        rbf.append(go(rb_q.at[there], rb_f.at[o - 1], device))

    rn[0].wait_recv()
    cores.append(to_partner((a + 3) % NEAR))
    rn[1].wait_recv()
    cores.append(to_partner((a + 1) % NEAR))
    rn[2].wait_recv()
    rn[3].wait_recv()
    cores.append(to_partner((a + 2) % NEAR))
    for copy in cores:
        copy.wait_recv()

    block = mem * NEAR * CORES * tok

    def turn(k, _):
        rt[k] = r_all[k].reshape(block, lanes).T
        return 0

    lax.fori_loop(0, X, turn, 0)

    def make_q(p, _):
        pair = pair_of(p)
        for k in range(X):
            q_all[p, k] = nn(rt[k], pair).astype(BF16)
        return 0

    lax.fori_loop(0, pairs, make_q, 0)

    lb_acc[...] = jnp.zeros_like(lb_acc)

    def of_q(g):
        at_row = pl.multiple_of(g * 2 * s8, 2 * s8)
        return q_all[:, :, pl.ds(at_row, 2 * s8), :].reshape(pairs * X * 2 * s8, 256)

    def make_lb(g, _):
        total = nt(of_q(4 * g), wb[4 * g])
        for u in range(1, 4):
            total = total + nt(of_q(4 * g + u), wb[4 * g + u])
        lb_acc[...] += total
        return 0

    lax.fori_loop(0, width // 8, make_lb, 0)
    acc = lb_acc[...].reshape(pairs * X, 2, s8, half)
    lb[...] = (jnp.where(lane < half // 2, acc[:, 0], acc[:, 1]) * scale).reshape(pairs, X, s8, half)
    lbx = [go(lb.at[:, (xi + dx) % X], lb_r.at[dx - 1], at(dx=dx)) for dx in range(1, X)]

    def make_s(g, _):
        there = (g % X) * CORES + g // X
        for u in range(2):
            found = nn(lpt2[...], of_q(2 * g + u)) * scale
            for d2 in range(2):
                top = d2 * 2 * width
                s_all[there, :, (2 * u + d2) * 128 : (2 * u + d2 + 1) * 128] = (
                    found[top : top + width, 0:128] + found[top + width : top + 2 * width, 128:256]
                ).astype(BF16)
        return 0

    lax.fori_loop(0, width // 4, make_s, 0)
    srs = []
    for o in range(1, level):
        there, device = peer(o)
        srs.append(go(s_all.at[there], s_rs.at[o - 1], device))

    def make_update(p, _):
        total = nn(r_all[0].reshape(block, lanes), t_all[p, 0])
        for k in range(1, X):
            total = total + nn(r_all[k].reshape(block, lanes), t_all[p, k])
        total = total * scale
        out[2 * p] = (total[:, 0:128] + bias[...]).astype(BF16)
        out[2 * p + 1] = (total[:, 128:256] + bias[...]).astype(BF16)
        return 0

    for copy in lbx:
        copy.wait_recv()
    lsum = (lb[:, xi] + lb_r[0] + lb_r[1] + lb_r[2]).reshape(pairs * s8, half)
    f1 = two_part(tn, lsum, even)
    f2 = two_part(tn, lsum, odd)
    left_slope = f1[0:width] + f1[2 * width : 3 * width] + f2[width : 2 * width] + f2[3 * width :]
    lax.fori_loop(0, pairs // 4, make_update, 0)

    for copy in srs:
        copy.wait_recv()
    stot = s_all[here].astype(F32)
    for k in range(level - 1):
        stot = stot + s_rs[k].astype(F32)
    s_n[...] = stot.reshape(NEAR, ring, stot.shape[1])
    sn = [
        go(s_n.at[(a + 1) % NEAR], s_nr.at[0], at(dz=1)),
        go(s_n.at[(a + 3) % NEAR], s_nr.at[1], at(dz=-1)),
        go(s_n.at[(a + 2) % NEAR], s_nr.at[2], at(dz=2)),
    ]

    for copy in rbf:
        copy.wait_recv()
    rb = rb_q[m].astype(F32)
    for k in range(ring - 1):
        rb = rb + rb_f[k].astype(F32)
    wide = jnp.where(pick, rb.reshape(tok, 1, lanes), 0.0).reshape(tok * s8, lanes)
    right_slope = jnp.sum(two_part(tn, wide, nb).reshape(width, s8, depth), axis=1)
    vtot = jnp.concatenate([left_slope, right_slope], axis=1)
    share = width // level
    for k in range(level):
        v_s[k] = vtot[k * share : (k + 1) * share]
    vrs = []
    for o in range(1, level):
        there, device = peer(o)
        vrs.append(go(v_s.at[there], v_rs.at[o - 1], device))

    for copy in sn:
        copy.wait_recv()
    tile = s_n[a] + s_nr[0] + s_nr[1] + s_nr[2]
    for k in range(share):
        s_f[:, k, :] = tile[:, k * 128 : (k + 1) * 128]
    sf = []
    for o in range(1, ring):
        there, device = far(o)
        sf.append(go(s_f.at[there], s_fr.at[o - 1], device))

    for copy in vrs:
        copy.wait_recv()
    vsum = v_s[here]
    for k in range(level - 1):
        vsum = vsum + v_rs[k]
    v_n[...] = vsum
    vn = [go(v_n, v_nr.at[k], at(dz=dz)) for k, dz in enumerate((1, -1, 2))]
    lax.fori_loop(pairs // 4, pairs // 2, make_update, 0)
    for copy in vn:
        copy.wait_recv()
    v_t[...] = v_n[...] + v_nr[0] + v_nr[1] + v_nr[2]
    vf = [go(v_t, v_fr.at[o - 1], far(o)[1]) for o in range(1, ring)]

    lax.fori_loop(pairs // 2, pairs, make_update, 0)
    leave = pltpu.make_async_copy(out, out_away, load_sem.at[8])
    leave.start()

    from_right = two_part(nt, wide, p2r)
    from_even = two_part(nt, lsum, p1e).reshape(pairs, 1, s8, depth)
    from_odd = two_part(nt, lsum, p1o).reshape(pairs, 1, s8, depth)
    from_left = jnp.concatenate([from_even, from_odd], axis=1).reshape(tok, s8, depth)
    scaled = (from_right.reshape(tok, s8, depth) + from_left) * gain[...][None]
    slope[...] = rs * (
        scaled
        - jnp.mean(scaled, axis=-1, keepdims=True)
        - xhat * jnp.mean(scaled * xhat, axis=-1, keepdims=True)
    )

    for copy in sf:
        copy.wait_recv()
    line = s_f[m]
    for k in range(ring - 1):
        line = line + s_fr[k]
    wslope[...] = line

    for copy in vf:
        copy.wait_recv()
    vline = v_t[...]
    for k in range(ring - 1):
        vline = vline + v_fr[k]
    v_f[here] = vline
    vag = [go(v_f.at[here], v_f.at[here], peer(o)[1]) for o in range(1, level)]
    for copy in vag:
        copy.wait_recv()
    for k in range(level):
        part = v_f[k]
        slope1[k * share : (k + 1) * share, :] = part[:, 0:depth]
        slope2[k * share : (k + 1) * share, :] = part[:, depth : 2 * depth]

    leave.wait()
    for copy in started:
        copy.wait_send()


PARTS = 4


def finish(*refs):
    count = (len(refs) - 2) // 3
    sources, targets, held = refs[:count], refs[count : 2 * count], refs[2 * count : 3 * count]
    in_sem, out_sem = refs[-2:]
    moves = []
    for k, (source, target, here) in enumerate(zip(sources, targets, held)):
        if k:
            moves.append((source, here, target))
            continue
        step = source.shape[0] // PARTS
        for n in range(PARTS):
            cut = pl.ds(n * step, step)
            moves.append((source.at[cut], here.at[cut], target.at[cut]))
    loads = [pltpu.make_async_copy(a, b, in_sem.at[n]) for n, (a, b, _) in enumerate(moves)]
    stores = [pltpu.make_async_copy(b, c, out_sem.at[n]) for n, (_, b, c) in enumerate(moves)]
    for copy in loads:
        copy.start()
    for load, store in zip(loads, stores):
        load.wait()
        store.start()
    for copy in stores:
        copy.wait()


def solution(mesh):
    X, Z = mesh.shape["cols"], mesh.shape["rows"] // CORES

    def local(feat, gain, offset, p1, p2, w, bias, cot):
        tok, s8, depth = feat.shape
        width = p1.shape[1]
        share = width // (CORES * X)
        pair_ch = w.shape[1]
        block = cot.shape[1]
        ring, mem, pairs = Z // NEAR, Z // X // NEAR, tok // 2
        lanes, half, seqs = width * s8, 4 * width, s8 * X
        level = CORES * X
        v = pltpu.VMEM
        scratch = [
            v(cot.shape, BF16),
            v(feat.shape, F32),
            v((1, depth), F32),
            v((1, depth), F32),
            v((width, depth), BF16),
            v((width, depth), BF16),
            v(w.shape, BF16),
            v((1, pair_ch), F32),
            v(cot.shape, BF16),
            v(w.shape, F32),
            v((width // 2, half, 2 * pair_ch), BF16),
            v((pairs, X, s8, half), F32),
            v((pairs * seqs * 2, half), BF16),
            v((half, pairs * seqs * 2), BF16),
            v((ring, tok, lanes), BF16),
            v((X, mem, NEAR, CORES, tok, lanes), BF16),
            v((X, lanes, block), BF16),
            v((pairs, X, lanes, 2 * pair_ch), BF16),
            v((pairs, X, lanes, 2 * pair_ch), BF16),
            v((X, mem, NEAR, CORES, tok, lanes), BF16),
            v((X, mem, NEAR, CORES, tok, lanes), F32),
            v((X, mem, NEAR, tok, lanes), BF16),
            v((NEAR, X, mem, tok, lanes), BF16),
            v((X, mem, tok, lanes), F32),
            v((NEAR - 1, X, mem, tok, lanes), BF16),
            v((X, mem, tok, lanes), BF16),
            v((ring, tok, lanes), BF16),
            v((ring - 1, tok, lanes), BF16),
            v((pairs * seqs * 2, half), F32),
            v((pairs, X, s8, half), F32),
            v((X - 1, pairs, s8, half), F32),
            v((level, width, share * pair_ch), BF16),
            v((level - 1, width, share * pair_ch), BF16),
            v((NEAR, ring, share * pair_ch), F32),
            v((NEAR - 1, ring, share * pair_ch), F32),
            v((ring, share, pair_ch), F32),
            v((ring - 1, share, pair_ch), F32),
            v((level, share, 2 * depth), F32),
            v((level - 1, share, 2 * depth), F32),
            v((share, 2 * depth), F32),
            v((NEAR - 1, share, 2 * depth), F32),
            v((share, 2 * depth), F32),
            v((ring - 1, share, 2 * depth), F32),
            v((level, share, 2 * depth), F32),
            pltpu.SemaphoreType.DMA((SEMS,)),
            pltpu.SemaphoreType.DMA((SEMS,)),
            pltpu.SemaphoreType.DMA((9,)),
        ]
        whole = pl.BlockSpec(memory_space=pltpu.VMEM)
        away = pl.BlockSpec(memory_space=pltpu.HBM)
        shapes = tuple(
            jax.ShapeDtypeStruct(dims, kind)
            for dims, kind in (
                (cot.shape, BF16),
                (feat.shape, F32),
                ((share, pair_ch), F32),
                ((width, depth), F32),
                ((width, depth), F32),
            )
        )
        found = pl.pallas_call(
            functools.partial(kernel, X, Z),
            out_shape=shapes,
            in_specs=[away] * 8,
            out_specs=(away,) + (whole,) * 4,
            scratch_shapes=scratch,
            compiler_params=pltpu.CompilerParams(
                collective_id=0, has_side_effects=True, vmem_limit_bytes=VMEM_BYTES
            ),
            name="outer_mean",
        )(feat, gain.reshape(1, -1), offset.reshape(1, -1), p1.T, p2.T, w, bias.reshape(1, -1), cot)
        done = pl.pallas_call(
            finish,
            out_shape=shapes,
            in_specs=[away] * 5,
            out_specs=(away,) * 5,
            scratch_shapes=[v(one.shape, one.dtype) for one in shapes]
            + [pltpu.SemaphoreType.DMA((PARTS + 4,))] * 2,
            compiler_params=pltpu.CompilerParams(vmem_limit_bytes=VMEM_BYTES),
            name="finish",
        )(*found)
        return (*done[:3], done[3].T, done[4].T)

    tokens = P(("groups", "rows"), "cols", None)
    return jax.shard_map(
        local,
        mesh=mesh,
        in_specs=(tokens, P(), P(), P(), P(), P(), P(), tokens),
        out_specs=(tokens, tokens, P(("groups", "rows", "cols"), None), P("groups", None), P("groups", None)),
        check_vma=False,
    )
```

time: 136 us -> 118 us (0.87)
  Pallas kernels: 128 us -> 117 us
  local copies, waits for them, and re-layouts: 7.8 us -> 0 us
    pallas_call x1 -> x2, Pallas kernels: 128 us -> 117 us  [the longest x1 115 us: local(): pl.pallas_call(functools.partial(kernel, X, Z), out_shape=shapes, in_spec...]
    unnamed x13 -> x0, local copies, waits for them, and re-layouts: 5.67 us -> none
    pallas_call x2 -> x0, local copies, waits for them, and re-layouts: 2.12 us -> none  [local(): pl.pallas_call(functools.partial(kernel, X, Z), out_shape=(shape(cot.shap...]
where the time goes in v2:
time: 118 us
  Pallas kernels  117 us (99%)
    pallas_call x1, Pallas kernels, local(): pl.pallas_call(functools.partial(kernel, X, Z), out_shape=shapes, in_spec...  115 us

profile of v2, /device:TPU:33, one launch (start us, length us, event | category | flops | bytes accessed | tf_op | source)
XLA Modules:
  0.0 117.5 jit_solution(17670561448851496642)
XLA Ops:
  0.6 114.8 %outer_mean.1 = (bf16[16,256,128]{2,1,0:T(8,128)(2,1)}, f32[16,8,64]{2,1,0:T(8,128)}, f32[4,128]{1,0:T(4,128)}, f32[32,64]{1,0:T(8,128)}, f32[32,64]{1,0:T(8,128)}) custom-call(f32[16,8,64]{2,1,0:T(8,128)} %feat_in.1, f32[1,64]{1,0:T(1,128)} %bitcast.9, f32[1,64]{1,0:T(1,128)} %bitcast.10, bf16[32,64]{1,0:T(8,128)(2,1)} %bitcast.7, bf16[32,64]{1,0:T(8,128)(2,1)} %bitcast.8, ...), custom_call_target="tpu_custom_call" | custom-call | tf_op jit(solution)/shard_map/outer_mean/pallas_call | solution.py:541
  115.5 2.1 %finish.1 = (bf16[16,256,128]{2,1,0:T(8,128)(2,1)}, f32[16,8,64]{2,1,0:T(8,128)}, f32[4,128]{1,0:T(4,128)}, f32[32,64]{1,0:T(8,128)}, f32[32,64]{1,0:T(8,128)}) custom-call(bf16[16,256,128]{2,1,0:T(8,128)(2,1)} %get-tuple-element.15.refs_0_, f32[16,8,64]{2,1,0:T(8,128)} %get-tuple-element.16.refs_1_, f32[4,128]{1,0:T(4,128)} %get-tuple-element.17.refs_2_, ...), custom_call_target="tpu_custom_call" | custom-call | tf_op jit(solution)/shard_map/finish/pallas_call | solution.py:552

commit v3 on v2

--- a/solution.py
+++ b/solution.py
@@ -11,7 +11,7 @@
 BF16 = jnp.bfloat16
 NEAR = 4
 CORES = 2
-SEMS = 96
+SEMS = 128
 VMEM_BYTES = 66 * 1000 * 1000
 
 
@@ -43,7 +43,7 @@
     out, feat, gain, offset, p1, p2, w, bias, cot, wf, wb, lf, lp2, lpt2, ring_r, r_all, rt, t_all, q_all,
     rb_bf, rb_own, rb_d, rb_n, rb_o, rb_r, rb_x, rb_q, rb_f,
     lb_acc, lb, lb_r, s_all, s_rs, s_n, s_nr, s_f, s_fr,
-    v_s, v_rs, v_n, v_nr, v_t, v_fr, v_f, send_sem, recv_sem, load_sem,
+    v_s, v_rs, v_t, v_fr, v_f, send_sem, recv_sem, load_sem,
 ):
     ring = Z // NEAR
     mem = Z // X // NEAR
@@ -96,12 +96,24 @@
     ]
     for copy in loads:
         copy.start()
-    steps = (1, -1, 2, -2, NEAR, -NEAR)
+    steps = (1, -1, 2, -2)
     barrier = pltpu.get_barrier_semaphore()
     for o in range(1, level):
         pl.semaphore_signal(barrier, inc=1, device_id=peer(o)[1], device_id_type=pl.DeviceIdType.MESH)
     for dz in steps:
         pl.semaphore_signal(barrier, inc=1, device_id=at(dz=dz), device_id_type=pl.DeviceIdType.MESH)
+    for o in range(1, ring):
+
+        @pl.when(m + o < ring)
+        def _(o=o):
+            pl.semaphore_signal(
+                barrier, inc=1, device_id=at(dz=NEAR * o), device_id_type=pl.DeviceIdType.MESH
+            )
+
+    @pl.when(m > 0)
+    def _():
+        pl.semaphore_signal(barrier, inc=1, device_id=at(dz=-NEAR), device_id_type=pl.DeviceIdType.MESH)
+
 
     for copy in loads[:5]:
         copy.wait()
@@ -143,20 +155,35 @@
         return 0
 
     lax.fori_loop(0, width // 2, spread, 0)
-    pl.semaphore_wait(barrier, level - 1 + len(steps))
-
-    def ring_up(buf, t):
-        q = (m - t + 1 + ring) % ring
-        return go(buf.at[q], buf.at[q], at(dz=NEAR))
-
-    def ring_down(buf, t):
-        q = (m + t - 1) % ring
-        return go(buf.at[q], buf.at[q], at(dz=-NEAR))
-
-    ups, downs = ring // 2, ring // 2 - 1
+    pl.semaphore_wait(barrier, level - 1 + len(steps) + m + 1 - m // (ring - 1))
+
+    base = SEMS - 2 * ring
+
+    def remote(k, q, dz):
+        return pltpu.make_async_remote_copy(
+            src_ref=ring_r.at[q], dst_ref=ring_r.at[q],
+            send_sem=send_sem.at[k], recv_sem=recv_sem.at[k],
+            device_id=at(dz=dz), device_id_type=pl.DeviceIdType.MESH,
+        )
+
+    def down(o):
+        return remote(base + o, m, -NEAR * o)
+
+    def up(j):
+        return remote(base + ring + j, m - j, NEAR)
 
     lefts = [go(lf.at[:, xi], lf.at[:, xi], at(dx=dx)) for dx in range(1, X)]
-    up, down = ring_up(ring_r, 1), ring_down(ring_r, 1)
+
+    @pl.when(m < ring - 1)
+    def _():
+        up(0).start()
+
+    for o in range(ring - 1, 0, -1):
+
+        @pl.when(m >= o)
+        def _(o=o):
+            down(o).start()
+
     for copy in lefts:
         copy.wait_recv()
 
@@ -178,13 +205,7 @@
             t_all[:, :, pl.ds(at_row, 2 * s8), :] = piece
         return 0
 
-    lax.fori_loop(0, width // 8, make_t, 0)
-
-    up.wait_recv()
-    up2 = ring_up(ring_r, 2)
-    down.wait_recv()
-    down2 = ring_down(ring_r, 2)
-    lax.fori_loop(width // 8, width // 4, make_t, 0)
+    lax.fori_loop(0, width // 4, make_t, 0)
     loads[6].wait()
     loads[7].wait()
 
@@ -203,10 +224,15 @@
     lax.fori_loop(0, X, make_rb, 0)
     rbd = go(rb_bf.at[:, :, :, 1 - core], rb_d, at(other=1 - core))
 
-    up2.wait_recv()
-    up3 = ring_up(ring_r, 3)
-    down2.wait_recv()
-    down3 = ring_down(ring_r, 3)
+    for j in range(ring - 1):
+
+        @pl.when(m > j)
+        def _(j=j):
+            remote(base + ring + j, m - 1 - j, NEAR).wait_recv()
+
+        @pl.when((m > j) & (m < ring - 1))
+        def _(j=j):
+            up(j + 1).start()
 
     rbd.wait_recv()
     for k in range(NEAR):
@@ -221,8 +247,27 @@
     ]
     rb_o[...] = rb_own[:, :, a, core] + rb_d[:, :, a].astype(F32)
 
-    up3.wait_recv()
-    up4 = ring_up(ring_r, 4)
+    for o in range(1, ring):
+
+        @pl.when(m + o < ring)
+        def _(o=o):
+            down(o).wait_recv()
+
+    rx = [
+        go(ring_r.at[pl.ds(((xi + dx) % X) * mem, mem)], r_all.at[xi, :, a, core], at(dx=dx))
+        for dx in range(1, X)
+    ]
+    r_all[xi, :, a, core] = ring_r[pl.ds(xi * mem, mem)]
+    partner = at(other=1 - core)
+
+    for copy in rx:
+        copy.wait_recv()
+    rn = [
+        go(r_all.at[:, :, a, core], r_all.at[:, :, a, core], at(dz=1)),
+        go(r_all.at[:, :, a, core], r_all.at[:, :, a, core], at(dz=-1)),
+        go(r_all.at[0:hx, :, a, core], r_all.at[0:hx, :, a, core], at(dz=2)),
+        go(r_all.at[hx:X, :, a, core], r_all.at[hx:X, :, a, core], at(dz=-2)),
+    ]
 
     for copy in rbn:
         copy.wait_recv()
@@ -233,24 +278,6 @@
         go(rb_x.at[(xi + dx) % X], rb_q.at[pl.ds(xi * mem, mem)], at(dx=dx)) for dx in range(1, X)
     ]
     rb_q[pl.ds(xi * mem, mem)] = rb_x[xi]
-
-    down3.wait_recv()
-    up4.wait_recv()
-    rx = [
-        go(ring_r.at[pl.ds(((xi + dx) % X) * mem, mem)], r_all.at[xi, :, a, core], at(dx=dx))
-        for dx in range(1, X)
-    ]
-    r_all[xi, :, a, core] = ring_r[pl.ds(xi * mem, mem)]
-    partner = at(other=1 - core)
-
-    for copy in rx:
-        copy.wait_recv()
-    rn = [
-        go(r_all.at[:, :, a, core], r_all.at[:, :, a, core], at(dz=1)),
-        go(r_all.at[:, :, a, core], r_all.at[:, :, a, core], at(dz=-1)),
-        go(r_all.at[0:hx, :, a, core], r_all.at[0:hx, :, a, core], at(dz=2)),
-        go(r_all.at[hx:X, :, a, core], r_all.at[hx:X, :, a, core], at(dz=-2)),
-    ]
 
     def to_partner(k):
         return go(r_all.at[:, :, k, core], r_all.at[:, :, k, core], partner)
@@ -343,20 +370,6 @@
     f1 = two_part(tn, lsum, even)
     f2 = two_part(tn, lsum, odd)
     left_slope = f1[0:width] + f1[2 * width : 3 * width] + f2[width : 2 * width] + f2[3 * width :]
-    lax.fori_loop(0, pairs // 4, make_update, 0)
-
-    for copy in srs:
-        copy.wait_recv()
-    stot = s_all[here].astype(F32)
-    for k in range(level - 1):
-        stot = stot + s_rs[k].astype(F32)
-    s_n[...] = stot.reshape(NEAR, ring, stot.shape[1])
-    sn = [
-        go(s_n.at[(a + 1) % NEAR], s_nr.at[0], at(dz=1)),
-        go(s_n.at[(a + 3) % NEAR], s_nr.at[1], at(dz=-1)),
-        go(s_n.at[(a + 2) % NEAR], s_nr.at[2], at(dz=2)),
-    ]
-
     for copy in rbf:
         copy.wait_recv()
     rb = rb_q[m].astype(F32)
@@ -369,9 +382,33 @@
     for k in range(level):
         v_s[k] = vtot[k * share : (k + 1) * share]
     vrs = []
-    for o in range(1, level):
-        there, device = peer(o)
-        vrs.append(go(v_s.at[there], v_rs.at[o - 1], device))
+    for n, dz in enumerate((0, 1, -1, 2)):
+        for o in range(level):
+            if n or o:
+                there = (here + o) % level
+                device = at(dz=dz)
+                device = {
+                    "rows": (device["rows"] // CORES) * CORES + there % CORES,
+                    "cols": there // CORES,
+                }
+                vrs.append(go(v_s.at[there], v_rs.at[n * level + o - 1], device))
+
+    for copy in srs:
+        copy.wait_recv()
+    stot = s_all[here].astype(F32)
+    for k in range(level - 1):
+        stot = stot + s_rs[k].astype(F32)
+    s_n[...] = stot.reshape(NEAR, ring, stot.shape[1])
+    sn = [
+        go(s_n.at[(a + 1) % NEAR], s_nr.at[0], at(dz=1)),
+        go(s_n.at[(a + 3) % NEAR], s_nr.at[1], at(dz=-1)),
+        go(s_n.at[(a + 2) % NEAR], s_nr.at[2], at(dz=2)),
+    ]
+
+    for copy in vrs:
+        copy.wait_recv()
+    v_t[...] = v_s[here] + jnp.sum(v_rs[...], axis=0)
+    vf = [go(v_t, v_fr.at[o - 1], far(o)[1]) for o in range(1, ring)]
 
     for copy in sn:
         copy.wait_recv()
@@ -383,20 +420,7 @@
         there, device = far(o)
         sf.append(go(s_f.at[there], s_fr.at[o - 1], device))
 
-    for copy in vrs:
-        copy.wait_recv()
-    vsum = v_s[here]
-    for k in range(level - 1):
-        vsum = vsum + v_rs[k]
-    v_n[...] = vsum
-    vn = [go(v_n, v_nr.at[k], at(dz=dz)) for k, dz in enumerate((1, -1, 2))]
-    lax.fori_loop(pairs // 4, pairs // 2, make_update, 0)
-    for copy in vn:
-        copy.wait_recv()
-    v_t[...] = v_n[...] + v_nr[0] + v_nr[1] + v_nr[2]
-    vf = [go(v_t, v_fr.at[o - 1], far(o)[1]) for o in range(1, ring)]
-
-    lax.fori_loop(pairs // 2, pairs, make_update, 0)
+    lax.fori_loop(0, pairs, make_update, 0)
     leave = pltpu.make_async_copy(out, out_away, load_sem.at[8])
     leave.start()
 
@@ -433,6 +457,23 @@
         slope2[k * share : (k + 1) * share, :] = part[:, depth : 2 * depth]
 
     leave.wait()
+
+    @pl.when(m < ring - 1)
+    def _():
+        up(0).wait_send()
+
+    for o in range(1, ring):
+
+        @pl.when(m >= o)
+        def _(o=o):
+            down(o).wait_send()
+
+    for j in range(ring - 1):
+
+        @pl.when((m > j) & (m < ring - 1))
+        def _(j=j):
+            up(j + 1).wait_send()
+
     for copy in started:
         copy.wait_send()
 
@@ -516,9 +557,7 @@
             v((ring, share, pair_ch), F32),
             v((ring - 1, share, pair_ch), F32),
             v((level, share, 2 * depth), F32),
-            v((level - 1, share, 2 * depth), F32),
-            v((share, 2 * depth), F32),
-            v((NEAR - 1, share, 2 * depth), F32),
+            v((NEAR * level - 1, share, 2 * depth), F32),
             v((share, 2 * depth), F32),
             v((ring - 1, share, 2 * depth), F32),
             v((level, share, 2 * depth), F32),

time: 118 us -> 130 us (1.10)
  Pallas kernels: 117 us -> 129 us
    pallas_call x1, Pallas kernels: 115 us -> 127 us  [local(): pl.pallas_call(functools.partial(kernel, X, Z), out_shape=shapes, in_spec...]
where the time goes in v3:
time: 130 us
  Pallas kernels  129 us (99%)
    pallas_call x1, Pallas kernels, local(): pl.pallas_call(functools.partial(kernel, X, Z), out_shape=shapes, in_spec...  127 us

profile of v3, /device:TPU:33, one launch (start us, length us, event | category | flops | bytes accessed | tf_op | source)
XLA Modules:
  0.0 129.7 jit_solution(16843969687386269846)
XLA Ops:
  0.6 127.0 %outer_mean.1 = (bf16[16,256,128]{2,1,0:T(8,128)(2,1)}, f32[16,8,64]{2,1,0:T(8,128)}, f32[4,128]{1,0:T(4,128)}, f32[32,64]{1,0:T(8,128)}, f32[32,64]{1,0:T(8,128)}) custom-call(f32[16,8,64]{2,1,0:T(8,128)} %feat_in.1, f32[1,64]{1,0:T(1,128)} %bitcast.9, f32[1,64]{1,0:T(1,128)} %bitcast.10, bf16[32,64]{1,0:T(8,128)(2,1)} %bitcast.7, bf16[32,64]{1,0:T(8,128)(2,1)} %bitcast.8, ...), custom_call_target="tpu_custom_call" | custom-call | tf_op jit(solution)/shard_map/outer_mean/pallas_call | solution.py:580
  127.6 2.1 %finish.1 = (bf16[16,256,128]{2,1,0:T(8,128)(2,1)}, f32[16,8,64]{2,1,0:T(8,128)}, f32[4,128]{1,0:T(4,128)}, f32[32,64]{1,0:T(8,128)}, f32[32,64]{1,0:T(8,128)}) custom-call(bf16[16,256,128]{2,1,0:T(8,128)(2,1)} %get-tuple-element.15.refs_0_, f32[16,8,64]{2,1,0:T(8,128)} %get-tuple-element.16.refs_1_, f32[4,128]{1,0:T(4,128)} %get-tuple-element.17.refs_2_, ...), custom_call_target="tpu_custom_call" | custom-call | tf_op jit(solution)/shard_map/finish/pallas_call | solution.py:591

commit v4 on v2

--- a/solution.py
+++ b/solution.py
@@ -11,7 +11,7 @@
 BF16 = jnp.bfloat16
 NEAR = 4
 CORES = 2
-SEMS = 96
+SEMS = 128
 VMEM_BYTES = 66 * 1000 * 1000
 
 
@@ -42,8 +42,8 @@
     out_away, slope, wslope, slope1, slope2,
     out, feat, gain, offset, p1, p2, w, bias, cot, wf, wb, lf, lp2, lpt2, ring_r, r_all, rt, t_all, q_all,
     rb_bf, rb_own, rb_d, rb_n, rb_o, rb_r, rb_x, rb_q, rb_f,
-    lb_acc, lb, lb_r, s_all, s_rs, s_n, s_nr, s_f, s_fr,
-    v_s, v_rs, v_n, v_nr, v_t, v_fr, v_f, send_sem, recv_sem, load_sem,
+    lb_acc, lb, lb_r, s_all, s_rs, s_n, s_nr, sv, sv_r,
+    v_s, v_rs, v_f, send_sem, recv_sem, load_sem,
 ):
     ring = Z // NEAR
     mem = Z // X // NEAR
@@ -263,7 +263,7 @@
     for copy in rbx:
         copy.wait_recv()
     rbf = []
-    for o in range(1, ring):
+    for o in sorted(range(1, ring), key=lambda o: -min(o, ring - o)):
         there, device = far(o)
         rbf.append(go(rb_q.at[there], rb_f.at[o - 1], device))
 
@@ -343,20 +343,6 @@
     f1 = two_part(tn, lsum, even)
     f2 = two_part(tn, lsum, odd)
     left_slope = f1[0:width] + f1[2 * width : 3 * width] + f2[width : 2 * width] + f2[3 * width :]
-    lax.fori_loop(0, pairs // 4, make_update, 0)
-
-    for copy in srs:
-        copy.wait_recv()
-    stot = s_all[here].astype(F32)
-    for k in range(level - 1):
-        stot = stot + s_rs[k].astype(F32)
-    s_n[...] = stot.reshape(NEAR, ring, stot.shape[1])
-    sn = [
-        go(s_n.at[(a + 1) % NEAR], s_nr.at[0], at(dz=1)),
-        go(s_n.at[(a + 3) % NEAR], s_nr.at[1], at(dz=-1)),
-        go(s_n.at[(a + 2) % NEAR], s_nr.at[2], at(dz=2)),
-    ]
-
     for copy in rbf:
         copy.wait_recv()
     rb = rb_q[m].astype(F32)
@@ -369,34 +355,46 @@
     for k in range(level):
         v_s[k] = vtot[k * share : (k + 1) * share]
     vrs = []
-    for o in range(1, level):
-        there, device = peer(o)
-        vrs.append(go(v_s.at[there], v_rs.at[o - 1], device))
+    for n, dz in enumerate((0, 1, -1, 2)):
+        for o in range(level):
+            if n or o:
+                there = (here + o) % level
+                device = at(dz=dz)
+                device = {
+                    "rows": (device["rows"] // CORES) * CORES + there % CORES,
+                    "cols": there // CORES,
+                }
+                vrs.append(go(v_s.at[there], v_rs.at[n * level + o - 1], device))
+
+    for copy in srs:
+        copy.wait_recv()
+    stot = s_all[here].astype(F32)
+    for k in range(level - 1):
+        stot = stot + s_rs[k].astype(F32)
+    s_n[...] = stot.reshape(NEAR, ring, stot.shape[1])
+    sn = [
+        go(s_n.at[(a + 1) % NEAR], s_nr.at[0], at(dz=1)),
+        go(s_n.at[(a + 3) % NEAR], s_nr.at[1], at(dz=-1)),
+        go(s_n.at[(a + 2) % NEAR], s_nr.at[2], at(dz=2)),
+    ]
+
+    for copy in vrs:
+        copy.wait_recv()
+    both_here = v_s[here] + jnp.sum(v_rs[...], axis=0)
+    for k in range(ring):
+        sv[k, share : 2 * share] = both_here
 
     for copy in sn:
         copy.wait_recv()
     tile = s_n[a] + s_nr[0] + s_nr[1] + s_nr[2]
     for k in range(share):
-        s_f[:, k, :] = tile[:, k * 128 : (k + 1) * 128]
-    sf = []
-    for o in range(1, ring):
+        sv[:, k, :] = tile[:, k * 128 : (k + 1) * 128]
+    svf = []
+    for o in sorted(range(1, ring), key=lambda o: -min(o, ring - o)):
         there, device = far(o)
-        sf.append(go(s_f.at[there], s_fr.at[o - 1], device))
-
-    for copy in vrs:
-        copy.wait_recv()
-    vsum = v_s[here]
-    for k in range(level - 1):
-        vsum = vsum + v_rs[k]
-    v_n[...] = vsum
-    vn = [go(v_n, v_nr.at[k], at(dz=dz)) for k, dz in enumerate((1, -1, 2))]
-    lax.fori_loop(pairs // 4, pairs // 2, make_update, 0)
-    for copy in vn:
-        copy.wait_recv()
-    v_t[...] = v_n[...] + v_nr[0] + v_nr[1] + v_nr[2]
-    vf = [go(v_t, v_fr.at[o - 1], far(o)[1]) for o in range(1, ring)]
-
-    lax.fori_loop(pairs // 2, pairs, make_update, 0)
+        svf.append(go(sv.at[there], sv_r.at[o - 1], device))
+
+    lax.fori_loop(0, pairs, make_update, 0)
     leave = pltpu.make_async_copy(out, out_away, load_sem.at[8])
     leave.start()
 
@@ -411,20 +409,12 @@
         - xhat * jnp.mean(scaled * xhat, axis=-1, keepdims=True)
     )
 
-    for copy in sf:
-        copy.wait_recv()
-    line = s_f[m]
-    for k in range(ring - 1):
-        line = line + s_fr[k]
-    wslope[...] = line
-
-    for copy in vf:
-        copy.wait_recv()
-    vline = v_t[...]
-    for k in range(ring - 1):
-        vline = vline + v_fr[k]
-    v_f[here] = vline
+    for copy in svf:
+        copy.wait_recv()
+    total = sv[m] + jnp.sum(sv_r[...], axis=0)
+    v_f[here] = total[share:]
     vag = [go(v_f.at[here], v_f.at[here], peer(o)[1]) for o in range(1, level)]
+    wslope[...] = total[:share]
     for copy in vag:
         copy.wait_recv()
     for k in range(level):
@@ -513,14 +503,10 @@
             v((level - 1, width, share * pair_ch), BF16),
             v((NEAR, ring, share * pair_ch), F32),
             v((NEAR - 1, ring, share * pair_ch), F32),
-            v((ring, share, pair_ch), F32),
-            v((ring - 1, share, pair_ch), F32),
+            v((ring, 2 * share, pair_ch), F32),
+            v((ring - 1, 2 * share, pair_ch), F32),
             v((level, share, 2 * depth), F32),
-            v((level - 1, share, 2 * depth), F32),
-            v((share, 2 * depth), F32),
-            v((NEAR - 1, share, 2 * depth), F32),
-            v((share, 2 * depth), F32),
-            v((ring - 1, share, 2 * depth), F32),
+            v((NEAR * level - 1, share, 2 * depth), F32),
             v((level, share, 2 * depth), F32),
             pltpu.SemaphoreType.DMA((SEMS,)),
             pltpu.SemaphoreType.DMA((SEMS,)),

time: 118 us -> 115 us (0.975)
  Pallas kernels: 117 us -> 114 us
    pallas_call x1, Pallas kernels: 115 us -> 112 us  [local(): pl.pallas_call(functools.partial(kernel, X, Z), out_shape=shapes, in_spec...]
where the time goes in v4:
time: 115 us; the launch traced here: 114 us
  Pallas kernels  114 us (99%)
    pallas_call x1, Pallas kernels, local(): pl.pallas_call(functools.partial(kernel, X, Z), out_shape=shapes, in_spec...  112 us

profile of v4, /device:TPU:33, one launch (start us, length us, event | category | flops | bytes accessed | tf_op | source)
XLA Modules:
  0.0 114.4 jit_solution(5711873203506465667)
XLA Ops:
  0.6 111.7 %outer_mean.1 = (bf16[16,256,128]{2,1,0:T(8,128)(2,1)}, f32[16,8,64]{2,1,0:T(8,128)}, f32[4,128]{1,0:T(4,128)}, f32[32,64]{1,0:T(8,128)}, f32[32,64]{1,0:T(8,128)}) custom-call(f32[16,8,64]{2,1,0:T(8,128)} %feat_in.1, f32[1,64]{1,0:T(1,128)} %bitcast.9, f32[1,64]{1,0:T(1,128)} %bitcast.10, bf16[32,64]{1,0:T(8,128)(2,1)} %bitcast.7, bf16[32,64]{1,0:T(8,128)(2,1)} %bitcast.8, ...), custom_call_target="tpu_custom_call" | custom-call | tf_op jit(solution)/shard_map/outer_mean/pallas_call | solution.py:527
  112.4 2.1 %finish.1 = (bf16[16,256,128]{2,1,0:T(8,128)(2,1)}, f32[16,8,64]{2,1,0:T(8,128)}, f32[4,128]{1,0:T(4,128)}, f32[32,64]{1,0:T(8,128)}, f32[32,64]{1,0:T(8,128)}) custom-call(bf16[16,256,128]{2,1,0:T(8,128)(2,1)} %get-tuple-element.15.refs_0_, f32[16,8,64]{2,1,0:T(8,128)} %get-tuple-element.16.refs_1_, f32[4,128]{1,0:T(4,128)} %get-tuple-element.17.refs_2_, ...), custom_call_target="tpu_custom_call" | custom-call | tf_op jit(solution)/shard_map/finish/pallas_call | solution.py:538

commit v5 on v4

--- a/solution.py
+++ b/solution.py
@@ -157,6 +157,10 @@
 
     lefts = [go(lf.at[:, xi], lf.at[:, xi], at(dx=dx)) for dx in range(1, X)]
     up, down = ring_up(ring_r, 1), ring_down(ring_r, 1)
+    up.wait_recv()
+    up2 = ring_up(ring_r, 2)
+    down.wait_recv()
+    down2 = ring_down(ring_r, 2)
     for copy in lefts:
         copy.wait_recv()
 
@@ -178,13 +182,7 @@
             t_all[:, :, pl.ds(at_row, 2 * s8), :] = piece
         return 0
 
-    lax.fori_loop(0, width // 8, make_t, 0)
-
-    up.wait_recv()
-    up2 = ring_up(ring_r, 2)
-    down.wait_recv()
-    down2 = ring_down(ring_r, 2)
-    lax.fori_loop(width // 8, width // 4, make_t, 0)
+    lax.fori_loop(0, width // 4, make_t, 0)
     loads[6].wait()
     loads[7].wait()
 
@@ -311,8 +309,10 @@
     lb[...] = (jnp.where(lane < half // 2, acc[:, 0], acc[:, 1]) * scale).reshape(pairs, X, s8, half)
     lbx = [go(lb.at[:, (xi + dx) % X], lb_r.at[dx - 1], at(dx=dx)) for dx in range(1, X)]
 
-    def make_s(g, _):
-        there = (g % X) * CORES + g // X
+    srs = []
+    for o in range(1, level + 1):
+        there, device = peer(o)
+        g = (there % CORES) * X + there // CORES
         for u in range(2):
             found = nn(lpt2[...], of_q(2 * g + u)) * scale
             for d2 in range(2):
@@ -320,13 +320,8 @@
                 s_all[there, :, (2 * u + d2) * 128 : (2 * u + d2 + 1) * 128] = (
                     found[top : top + width, 0:128] + found[top + width : top + 2 * width, 128:256]
                 ).astype(BF16)
-        return 0
-
-    lax.fori_loop(0, width // 4, make_s, 0)
-    srs = []
-    for o in range(1, level):
-        there, device = peer(o)
-        srs.append(go(s_all.at[there], s_rs.at[o - 1], device))
+        if o < level:
+            srs.append(go(s_all.at[there], s_rs.at[o - 1], device))
 
     def make_update(p, _):
         total = nn(r_all[0].reshape(block, lanes), t_all[p, 0])

time: 115 us -> 114 us (level)
  no operation moved by 1% of the time
where the time goes in v5:
time: 114 us
  Pallas kernels  113 us (99%)
    pallas_call x1, Pallas kernels, local(): pl.pallas_call(functools.partial(kernel, X, Z), out_shape=shapes, in_spec...  111 us

profile of v5, /device:TPU:33, one launch (start us, length us, event | category | flops | bytes accessed | tf_op | source)
XLA Modules:
  0.0 113.8 jit_solution(10843201426404727851)
XLA Ops:
  0.6 111.1 %outer_mean.1 = (bf16[16,256,128]{2,1,0:T(8,128)(2,1)}, f32[16,8,64]{2,1,0:T(8,128)}, f32[4,128]{1,0:T(4,128)}, f32[32,64]{1,0:T(8,128)}, f32[32,64]{1,0:T(8,128)}) custom-call(f32[16,8,64]{2,1,0:T(8,128)} %feat_in.1, f32[1,64]{1,0:T(1,128)} %bitcast.9, f32[1,64]{1,0:T(1,128)} %bitcast.10, bf16[32,64]{1,0:T(8,128)(2,1)} %bitcast.7, bf16[32,64]{1,0:T(8,128)(2,1)} %bitcast.8, ...), custom_call_target="tpu_custom_call" | custom-call | tf_op jit(solution)/shard_map/outer_mean/pallas_call | solution.py:522
  111.7 2.1 %finish.1 = (bf16[16,256,128]{2,1,0:T(8,128)(2,1)}, f32[16,8,64]{2,1,0:T(8,128)}, f32[4,128]{1,0:T(4,128)}, f32[32,64]{1,0:T(8,128)}, f32[32,64]{1,0:T(8,128)}) custom-call(bf16[16,256,128]{2,1,0:T(8,128)(2,1)} %get-tuple-element.15.refs_0_, f32[16,8,64]{2,1,0:T(8,128)} %get-tuple-element.16.refs_1_, f32[4,128]{1,0:T(4,128)} %get-tuple-element.17.refs_2_, ...), custom_call_target="tpu_custom_call" | custom-call | tf_op jit(solution)/shard_map/finish/pallas_call | solution.py:533
